TPU v7x, 32 devices: a 4x4x1 block of a 4x4x8 slice. The times are simulated.
32 devices in a mesh: dp: 2 (over z, core), tp: 16 (over x, y).
Axes of the slice: x: 4, y: 4, z: 1, core: 2. Of those that a mesh axis runs over, the one named last changes fastest.
The devices are a block of a 4x4x8 slice.
Arguments:
- x: bfloat16 [8192, 4096], P(('dp', 'tp')), parts along dimension 0
- dy: bfloat16 [8192, 4096], P(('dp', 'tp')), parts along dimension 0
- gate: bfloat16 [8192, 16384], P('dp', 'tp'), parts along dimension 0
- up: bfloat16 [8192, 16384], P('dp', 'tp'), parts along dimension 0
- w_gate: bfloat16 [4096, 16384], P(None, 'tp')
- w_up: bfloat16 [4096, 16384], P(None, 'tp')
- w_down: bfloat16 [16384, 4096], P('tp')
Outputs:
- output 1: bfloat16 [8192, 4096], P(('dp', 'tp')), parts along dimension 0
- output 2: bfloat16 [8192, 16384], P('dp', 'tp'), parts along dimension 0
- output 3: bfloat16 [8192, 16384], P('dp', 'tp'), parts along dimension 0
- output 4: bfloat16 [32768, 4096], P(('dp', 'tp')), parts along dimension 0
There are 2 independent parts. A program takes and returns all parts, laid end to end along the dimension named above; an argument that names none is the same for every part.
All inputs are finite; a program needn't handle non-finite values.
Results may differ from a plain program's by a relative error of at most 0.012.
Values are sent between devices in bfloat16 or wider.
A program may use at most 768 MiB of HBM per device.

v0:
```python
import jax
import jax.numpy as jnp


def act(gate, up):
    return jax.nn.silu(gate) * up


def solution(mesh):
    def step(x, dy, gate, up, w_gate, w_up, w_down):
        hidden, back = jax.vjp(act, gate.astype(jnp.float32), up.astype(jnp.float32))
        d_hidden = jnp.dot(dy, w_down.T, preferred_element_type=jnp.float32)
        d_gate, d_up = (g.astype(jnp.bfloat16) for g in back(d_hidden))
        dx = jnp.dot(d_gate, w_gate.T) + jnp.dot(d_up, w_up.T)
        groups = mesh.shape["dp"]

        def by_group(a, b):
            a, b = (t.reshape(groups, -1, t.shape[-1]) for t in (a, b))
            product = jnp.einsum("gta,gtb->gab", a, b, preferred_element_type=jnp.float32)
            return product.astype(jnp.bfloat16).reshape(-1, b.shape[-1])

        return dx, by_group(x, d_gate), by_group(x, d_up), by_group(hidden.astype(jnp.bfloat16), dy)

    return step
```

profile of v0, /device:TPU:97, one launch (start us, length us, event | category | flops | bytes accessed | tf_op | source)
XLA Modules:
  0.0 598.8 jit_solution(12106543443896386839)
XLA Ops:
  7.2 0.1 all-gather.11.cloned.1.call-start
  7.2 0.7 all-gather.11.cloned.1.call-update
  8.0 0.1 all-gather.13.cloned.1.call-start
  8.0 0.7 all-gather.13.cloned.1.call-update
  8.8 0.1 reduce-scatter.4.cloned.1.call-start
  8.9 196.6 %all-gather.11.cloned.1.call-done = bf16[4096,4096]{1,0:T(8,128)(2,1)} async-done(((bf16[256,4096]{1,0:T(8,128)(2,1)}), bf16[4096,4096]{1,0:T(8,128)(2,1)}) %all-gather.11.cloned.1.call-update) | async-done | bytes 33554448 | tf_op args[1]
  205.5 48.8 %fusion.6 = (bf16[4096,1024]{1,0:T(8,128)(2,1)}, f32[4096,1024]{1,0:T(8,128)}) fusion(bf16[4096,1024]{1,0:T(8,128)(2,1)} %param.3, bf16[4096,1024]{1,0:T(8,128)(2,1)} %param.2, bf16[4096,4096]{1,0:T(8,128)(2,1)} %all-gather.11.cloned.1.call-done, bf16[1024,4096]{1,0:T(8,128)(2,1)} %param.1), kind=kOutput, calls=%fused_computation.13 | convolution fusion | flops 34414264320 | bytes 83886080 | tf_op jit(solution)/dot_general | solution.py:12
  254.2 43.2 %fusion.13 = bf16[4096,4096]{1,0:T(8,128)(2,1)} fusion(bf16[4096,1024]{1,0:T(8,128)(2,1)} %get-tuple-element.4, bf16[4096,1024]{1,0:T(8,128)(2,1)} %param.4), kind=kOutput, calls=%fused_computation.20 | convolution fusion | flops 34359738368 | bytes 50331648 | tf_op jit(solution)/dot_general | solution.py:14
  297.5 45.4 %convolution_add_fusion = bf16[4096,4096]{1,0:T(8,128)(2,1)} fusion(bf16[4096,4096]{1,0:T(8,128)(2,1)} %fusion.13, bf16[4096,1024]{1,0:T(8,128)(2,1)} %param.5, f32[4096,1024]{1,0:T(8,128)} %get-tuple-element.5, bf16[4096,1024]{1,0:T(8,128)(2,1)} %param.3), kind=kOutput, calls=%fused_computation.4 | convolution fusion | flops 34405875712 | bytes 100663296 | tf_op jit(solution)/dot_general | solution.py:14
  342.9 0.1 reduce-scatter.4.cloned.1.call-update
  342.9 56.0 %all-gather.13.cloned.1.call-done = bf16[4096,4096]{1,0:T(8,128)(2,1)} async-done(((bf16[256,4096]{1,0:T(8,128)(2,1)}), bf16[4096,4096]{1,0:T(8,128)(2,1)}) %all-gather.13.cloned.1.call-update) | async-done | bytes 33554448 | tf_op jit(solution)/reshape | solution.py:18
  398.9 53.9 %convert_bitcast_fusion = bf16[4096,1024]{0,1:T(8,128)(2,1)} fusion(bf16[4096,4096]{1,0:T(8,128)(2,1)} %all-gather.13.cloned.1.call-done, f32[4096,1024]{1,0:T(8,128)} %get-tuple-element.5, bf16[4096,1024]{1,0:T(8,128)(2,1)} %param.3), kind=kOutput, calls=%fused_computation.16 | convolution fusion | flops 34393292800 | bytes 67108864 | tf_op jit(solution)/gta,gtb->gab/dot_general | solution.py:19
  452.8 11.9 %copy.1 = bf16[4096,1024]{1,0:T(8,128)(2,1)} copy(bf16[4096,1024]{0,1:T(8,128)(2,1)} %convert_bitcast_fusion) | data formatting | bytes 16777216
  464.7 43.6 %convert_bitcast_fusion.1 = bf16[4096,1024]{0,1:T(8,128)(2,1)} fusion(bf16[4096,1024]{1,0:T(8,128)(2,1)} %get-tuple-element.4, bf16[4096,4096]{1,0:T(8,128)(2,1)} %all-gather.13.cloned.1.call-done), kind=kOutput, calls=%fused_computation.17 | convolution fusion | flops 34363932672 | bytes 50331648 | tf_op jit(solution)/gta,gtb->gab/dot_general | solution.py:19
  508.3 11.9 %copy = bf16[4096,1024]{1,0:T(8,128)(2,1)} copy(bf16[4096,1024]{0,1:T(8,128)(2,1)} %convert_bitcast_fusion.1) | data formatting | bytes 16777216
  520.3 53.7 %fusion.9 = bf16[1024,4096]{1,0:T(8,128)(2,1)} fusion(bf16[4096,4096]{1,0:T(8,128)(2,1)} %all-gather.11.cloned.1.call-done, bf16[4096,1024]{1,0:T(8,128)(2,1)} %param.2, bf16[4096,1024]{1,0:T(8,128)(2,1)} %param.3), kind=kOutput, calls=%fused_computation.18 | convolution fusion | flops 34397487104 | bytes 58720256 | tf_op jit(solution)/gta,gtb->gab/dot_general | solution.py:19
  574.0 18.1 %reduce-scatter.4.cloned.1.call-done = bf16[256,4096]{1,0:T(8,128)(2,1)} async-done(((bf16[4096,4096]{1,0:T(8,128)(2,1)}), bf16[256,4096]{1,0:T(8,128)(2,1)}) %reduce-scatter.4.cloned.1.call-update) | async-done | bytes 2097168
Async XLA Ops:
  7.2 198.3 %all-gather.11.cloned.1.call-start = ((), (), s32[]{:S(2)}) async-start(), calls=%async_computation.1 | async-start | bytes 35651584 | tf_op args[1]
  8.0 391.0 %all-gather.13.cloned.1.call-start = ((), (), s32[]{:S(2)}) async-start(), calls=%async_computation.2 | async-start | bytes 35651584 | tf_op jit(solution)/reshape | solution.py:18
  8.8 583.3 %reduce-scatter.4.cloned.1.call-start = ((), (), s32[]{:S(2)}) async-start(), calls=%async_computation.3 | async-start | bytes 35651584
Sparse Core Ops, SparseCore 0:
  10.0 195.4 all-gather.10
  207.4 191.4 all-gather.12
  402.9 189.1 reduce-scatter.3
where the time goes:
time: 604 us; the launch traced here: 599 us
  matrix products  289 us (48%)
  waiting for transfers between devices  272 us (45%)
  local copies, waits for them, and re-layouts  23.9 us (4%)
  between operations  14 us (2%)
    unnamed x5, waiting for transfers between devices  216 us
    dot_general x3, matrix products, by_group(): jnp.einsum('gta,gtb->gab', a, b, preferred_element_type=jnp.float32)  151 us
    dot_general x2, matrix products, step(): dx = jnp.dot(d_gate, w_gate.T) + jnp.dot(d_up, w_up.T)  88.6 us
    reshape x1, waiting for transfers between devices, by_group(): a, b = (t.reshape(groups, -1, t.shape[-1]) for t in (a, b))  56 us
    dot_general x1, matrix products, step(): d_hidden = jnp.dot(dy, w_down.T, preferred_element_type=jnp.float32)  48.8 us
    unnamed x2, local copies, waits for them, and re-layouts  23.9 us
  transfers between devices with their start and end apart: 3, of which 3 were waited for; matrix products, arithmetic and copies ran while one was open for 52% of the time, Pallas kernels for 0%

commit v1 on v0

v1 whole, which is shorter than its diff:
```python
import functools
import math

import jax
import jax.numpy as jnp
from jax import lax
from jax.experimental import pallas as pl
from jax.experimental.pallas import tpu as pltpu
from jax.sharding import PartitionSpec as P

MESH = pl.DeviceIdType.MESH
BF16 = jnp.bfloat16
F32 = jnp.float32
NT = (((1,), (1,)), ((), ()))
TN = (((0,), (0,)), ((), ()))
BOTH = (0, 1)
SUB = 2
PIECES = tuple(range(SUB))

X_AFTER = 9
X_START = (0, 6)
DURING_CHUNKS = ((0, 2, 2, 2), (0, 3, 4, 6), (0, 4, 6, 8), (0, 5, 8, 10), (0, 6, 10, 10), (1, 0, 12, 14))
DURING_DOWN = ((1, 1, 5, 6), (1, 2, 14, 15))
DURING_DX = ((1, 3, 6, 7), (1, 4, 15, 16), (1, 5, 25, 26))
SUMS_AT = (29, 18)


scope = jax.named_scope


def dot(a, b, dims):
    return lax.dot_general(a, b, dims, preferred_element_type=F32)


def kernel(
    side,
    x_in, dy_in, gate, up, wg, wu, wd,
    dx, og, ou, od, xg, dyg, cg, cu, cwg, cwu, cwd, dxp, dxr, rsl, crs,
    dgu, hid, wb, gu, out, xf, rin, rpx, rpr, rso,
    rsend, rrecv, dsend, drecv, csend, crecv, gsend, grecv,
    wsem, lsem, osem, orecv, xfs, xbs, drr, rss, rsr, rls, crr, csem,
):
    n = side
    ring_len = 2 * n
    rb, d_model = x_in.shape
    tok, ff = gate.shape
    hb = rb // 2
    fh = ff // 2
    kd = d_model // 2
    piece = hb // SUB
    blocks = tok // rb
    cq = d_model // 4

    t = lax.axis_index("tp")
    dp = lax.axis_index("dp")
    c = lax.rem(dp, 2)
    x = t // n
    y = lax.rem(t, n)
    s = lax.rem(x + y, n)
    team = s // 2
    odd = lax.rem(s, 2)
    swap = lax.rem(c + team, 2)
    stay = 1 - swap
    pdp = dp + 1 - 2 * c

    def on_stay(f):
        pl.when(stay == 1)(f)

    def on_swap(f):
        pl.when(swap == 1)(f)

    def wrap(v):
        return lax.rem(v + 2 * n, n)

    def wr(v):
        return lax.rem(v + 4 * ring_len, ring_len)

    def neighbours(x, y, odd):
        sg = 2 * odd - 1
        cx = wrap(x + sg) * n + y
        cy = x * n + wrap(y + sg)
        rx = wrap(x - sg) * n + y
        ry = x * n + wrap(y - sg)
        return cx, cy, rx * (1 - odd) + ry * odd, ry * (1 - odd) + rx * odd

    cx, cy, nxt, prv = neighbours(x, y, odd)
    links = (cx, cy)
    r = wr(2 * x - odd)

    def stay_f(q, team):
        q = wr(q)
        o = lax.rem(q, 2)
        bx = lax.rem((q + o) // 2, n)
        return bx * n + wrap(2 * team + o - bx)

    def swap_f(q, team):
        q = wr(q)
        o = lax.rem(q, 2)
        bx = lax.rem((q + 3 * o) // 2, n)
        return bx * n + wrap(2 * (1 - team) + (1 - o) - bx)

    def blk_f(q_stay, q_swap):
        return stay_f(q_stay, team) * stay + swap_f(q_swap, team) * swap

    def send_blk(dn, i):
        if dn == 0:
            return blk_f(r - i, r - i - (1 if i >= 1 else 0))
        return blk_f(r + i, r - 2 if i == 0 else r - 1 + i)

    def arr_blk(dn, k):
        if dn == 0:
            return blk_f(r - 1 - k, r - 1 if k == 0 else r - 2 - k)
        return blk_f(r + 1 + k, r - 1 if k == 0 else r + k)

    def chunk(j, team, r, t, cx, cy):
        k = jnp.maximum(j - 3, 0) // 2
        sw = jnp.where((j == 1) | (j == 2) | ((j >= 4) & (lax.rem(j, 2) == 0)), 1, 0)
        first = jnp.where(k == 0, 1, 0)
        st_a = jnp.where(j == 0, t, stay_f(r - 1 - k, team))
        st_b = jnp.where(j == 0, t, stay_f(r + 1 + k, team))
        entry = jnp.where(j == 1, cx, cy)
        sw_a = jnp.where(j < 3, entry, swap_f(r - 2 - k + first, team))
        sw_b = jnp.where(j < 3, entry, swap_f(r + k - first, team))
        return sw_a * sw + st_a * (1 - sw), sw_b * sw + st_b * (1 - sw), sw, k

    def al(v, m):
        return pl.multiple_of(v, m)

    bar = pltpu.get_barrier_semaphore()
    peers = ((dp, nxt), (dp, prv), (pdp, t), (pdp, cx), (pdp, cy))
    for p, f in peers:
        pl.semaphore_signal(bar, inc=1, device_id={"dp": p, "tp": f}, device_id_type=MESH)
    pl.semaphore_wait(bar, len(peers))

    ins = (dy_in, x_in)
    gath = (dyg, xg)
    nbr = (nxt, prv)

    def remote(src, dst, ssem, rsem, to_dp, to_tp):
        return pltpu.make_async_remote_copy(
            src, dst, ssem, rsem, device_id={"dp": to_dp, "tp": to_tp}, device_id_type=MESH
        )

    def rows_of(blk, dn, u):
        return pl.ds(al(blk * rb + (dn * hb + u * piece), piece), piece)

    def ring(a, dn, i, u, blk, own=False):
        dst = gath[a].at[rows_of(blk, dn, u)]
        src = ins[a].at[pl.ds(dn * hb + u * piece, piece)] if own else dst
        return remote(src, dst, rsend.at[a, dn, i, u], rrecv.at[a, dn, i, u], dp, nbr[dn])

    def d2d(a, dn, i, u, blk, own=False):
        dst = gath[a].at[rows_of(blk, dn, u)]
        src = ins[a].at[pl.ds(dn * hb + u * piece, piece)] if own else dst
        return remote(src, dst, dsend.at[a, dn, i, u], drecv.at[a, dn, i, u], pdp, t)

    def cross(l, j):
        cols = pl.ds(l * fh, fh)
        if j in (0, 1, 3, 4):
            a, h = (0, j) if j < 2 else (1, j - 3)
            src = ins[a].at[pl.ds(h * hb, hb)]
            dst = gath[a].at[pl.ds(al(t * rb + h * hb, hb), hb)]
        elif j == 2:
            src, dst = wd.at[cols], cwd.at[cols]
        elif j < 13:
            q = (j - 5) // 2
            w, cw = ((wg, cwg), (wu, cwu))[(j - 5) % 2]
            rows = pl.ds(q * cq, cq)
            src, dst = w.at[rows, cols], cw.at[rows, cols]
        else:
            src, dst = cwd.at[cols], od.at[cols]
        return remote(src, dst, csend.at[l, j], crecv.at[l, j], pdp, links[l])

    def cross_gu(l, j, h, a, f):
        rows = pl.ds(al(f * rb + h * hb, hb), hb)
        cols = pl.ds(l * fh, fh)
        src, dst = ((gate, cg), (up, cu))[a]
        return remote(src.at[rows, cols], dst.at[rows, cols], gsend.at[l, j, h, a], grecv.at[l, j, h, a], pdp, links[l])

    def their_chunk(l, j):
        f = links[l]
        fx, fy = f // n, lax.rem(f, n)
        f_odd = 1 - odd
        f_cx, f_cy, _, _ = neighbours(fx, fy, f_odd)
        f_a, f_b, _, _ = chunk(j, 1 - team, wr(2 * fx - f_odd), f, f_cx, f_cy)
        return f_a, f_b

    def cross_chunks(lo, hi):
        @pl.loop(lo, hi)
        def _(j):
            for l in BOTH:
                halves = their_chunk(l, j)
                for h in BOTH:
                    for a in BOTH:
                        cross_gu(l, j, h, a, halves[h]).start()

    @scope("ring_start")
    def ring_start(a):
        @on_stay
        def _():
            for u in PIECES:
                for dn in BOTH:
                    ring(a, dn, 0, u, t, own=True).start()
            for u in PIECES:
                for dn in BOTH:
                    d2d(a, dn, 7, u, t, own=True).start()

        @on_swap
        def _():
            for l in BOTH:
                for h in BOTH:
                    cross(l, 3 * a + h).wait_recv()
            for i in BOTH:
                for u in PIECES:
                    for dn in BOTH:
                        ring(a, dn, i, u, send_blk(dn, i)).start()
            for l in BOTH:
                for u in PIECES:
                    for dn in BOTH:
                        d2d(a, dn, 6 + l, u, links[l]).start()

    def ring_step(a, k):
        def body():
            for u in PIECES:
                for dn in BOTH:
                    b = arr_blk(dn, k)
                    ring(a, dn, k, u, b).wait_recv()

                    def forward():
                        ring(a, dn, k + 1, u, b).start()

                    if 1 <= k <= 4:
                        forward()
                    elif k < 6:
                        on_stay(forward)
                    d2d(a, dn, k, u, b).start()

        with scope(f"ring_{a}_{k}"):
            if k == 6:
                on_stay(body)
            else:
                body()

    def ring_steps(table, i):
        for a, k, on_stay_at, on_swap_at in table:

            @pl.when(i == on_stay_at * stay + on_swap_at * swap)
            def _():
                ring_step(a, k)
                if (a, k) == X_START:
                    ring_start(1)

    def bounce(a, h, kb, out_):
        vm = dgu.at[pl.ds((2 * a + kb) * rb + h * hb, hb), :]
        cols = pl.ds(kb * kd, kd)
        if out_:
            return pltpu.make_async_copy(vm, gath[a].at[pl.ds(al(t * rb + h * hb, hb), hb), cols], lsem.at[0, h, 2 * a + kb])
        return pltpu.make_async_copy(ins[a].at[pl.ds(h * hb, hb), cols], vm, lsem.at[0, h, 2 * a + kb])

    def wd_load(src, kb):
        return pltpu.make_async_copy(src.at[:, pl.ds(kb * kd, kd)], wb.at[1, pl.ds(kb * ff, ff), :], wsem.at[kb])

    early = blocks // 2

    @on_swap
    def _():
        for j in range(3):
            for l in BOTH:
                cross(l, j).start()
        cross_chunks(0, early)

    @on_stay
    def _():
        for a in BOTH:
            for h in BOTH:
                for kb in BOTH:
                    bounce(a, h, kb, False).start()
        for kb in BOTH:
            wd_load(wd, kb).start()

    ring_start(0)

    @on_stay
    def _():
        for out_ in (False, True):
            for a in BOTH:
                for h in BOTH:
                    for kb in BOTH:
                        bounce(a, h, kb, out_).wait()
                        if not out_:
                            bounce(a, h, kb, True).start()

    ring_step(0, 0)

    @on_swap
    def _():
        cross_chunks(early, X_AFTER)
        for j in (3, 4):
            for l in BOTH:
                cross(l, j).start()
        cross_chunks(X_AFTER, blocks)
        for j in range(5, 13):
            for l in BOTH:
                cross(l, j).start()

    ring_step(0, 1)

    @on_swap
    def _():
        for l in BOTH:
            cross(l, 2).wait_recv()
        for kb in BOTH:
            wd_load(cwd, kb).start()

    def chunk_load(j, slot, h, what, f):
        rows = pl.ds(al(f * rb + h * hb, hb), hb)
        sem = lsem.at[slot, h, what]
        if what < 2:
            dst = wb.at[0, pl.ds(al(slot * 2 * rb + what * rb + h * hb, hb), hb), :]
            return pltpu.make_async_copy(dyg.at[rows, pl.ds(what * kd, kd)], dst, sem)
        dst = gu.at[slot, what % 2, pl.ds(h * hb, hb), :]
        src = ((gate, up), (cg, cu))[what // 4][what % 2]
        return pltpu.make_async_copy(src.at[rows, :], dst, lsem.at[slot, h, 2 + what % 2])

    @scope("chunk_start")
    def chunk_start(j):
        slot = lax.rem(j, 2)
        f_a, f_b, sw, k = chunk(j, team, r, t, cx, cy)
        halves = (f_a, f_b)

        @pl.when(sw != swap)
        def _():
            idx = jnp.where(j == 0, 7, jnp.where(j < 3, 5 + j, k))
            for dn in BOTH:
                for u in PIECES:
                    d2d(0, dn, idx, u, halves[dn]).wait_recv()

        for h in BOTH:
            for kb in BOTH:
                chunk_load(j, slot, h, kb, halves[h]).start()

        @on_stay
        def _():
            for h in BOTH:
                for a in BOTH:
                    chunk_load(j, slot, h, 2 + a, halves[h]).start()

        @on_swap
        def _():
            for l in BOTH:
                for h in BOTH:
                    for a in BOTH:
                        cross_gu(l, j, h, a, halves[h]).wait_recv()
            for h in BOTH:
                for a in BOTH:
                    chunk_load(j, slot, h, 4 + a, halves[h]).start()

    @scope("chunk")
    def chunk_compute(j):
        slot = lax.rem(j, 2)
        f_a, f_b, _, _ = chunk(j, team, r, t, cx, cy)
        halves = (f_a, f_b)
        for h in BOTH:
            for what in range(4):
                chunk_load(j, slot, h, what, halves[h]).wait()
        for nt in BOTH:
            cols = pl.ds(nt * fh, fh)
            lhs = al(slot * 2 * rb, 2 * rb)
            dh = dot(wb[0, pl.ds(lhs, rb), :], wb[1, pl.ds(nt * fh, fh), :], NT)
            dh += dot(wb[0, pl.ds(lhs + rb, rb), :], wb[1, pl.ds(ff + nt * fh, fh), :], NT)
            g = gu[slot, 0, :, cols].astype(F32)
            u = gu[slot, 1, :, cols].astype(F32)
            sig = jax.nn.sigmoid(g)
            act = g * sig
            d_up = (dh * act).astype(BF16)
            d_gate = ((dh * u) * (sig * (1.0 + g * (1.0 - sig)))).astype(BF16)
            hidden = (act * u).astype(BF16)
            for h in BOTH:
                rows = pl.ds(al(halves[h] * rb + h * hb, hb), hb)
                part = slice(h * hb, (h + 1) * hb)
                dgu[rows, nt * fh : (nt + 1) * fh] = d_gate[part]
                dgu[rows, ff + nt * fh : ff + (nt + 1) * fh] = d_up[part]
                hid[rows, nt * fh : (nt + 1) * fh] = hidden[part]

    chunk_start(0)

    @on_stay
    def _():
        chunk_start(1)

    for kb in BOTH:
        wd_load(wd, kb).wait()

    @pl.loop(0, blocks)
    def _(j):
        chunk_compute(j)
        ring_steps(DURING_CHUNKS, j)

        @pl.when(j + 1 + stay < blocks)
        def _():
            chunk_start(j + 1 + stay)

    half = tok // 2

    def dy_cols(q, slot, th):
        return pltpu.make_async_copy(
            dyg.at[pl.ds(th * half, half), pl.ds(al(q * cq, cq), cq)],
            wb.at[slot, :, pl.ds(th * cq, cq)],
            wsem.at[2 * slot + th],
        )

    def dd_out(i, to):
        rows = pl.ds(al(lax.rem(i, 4) * rb, rb), rb)
        cols = pl.ds(al((i // 4) * cq, cq), cq)
        o = lax.rem(i, 4)
        return pltpu.make_async_copy(out.at[o, 0], to.at[rows, cols], osem.at[o, 0, 0])

    for q in BOTH:
        for th in BOTH:
            dy_cols(q, q, th).start()

    @scope("dw_down")
    def down_tile(i):
        q = i // 4
        ft = lax.rem(i, 4)
        slot = lax.rem(q, 2)

        @pl.when(ft == 0)
        def _():
            for th in BOTH:
                dy_cols(q, slot, th).wait()

            @pl.when((q == 1) | (q == 2))
            def _():
                for th in BOTH:
                    dy_cols(q + 1, 1 - slot, th).start()

        @pl.when(i >= 4)
        def _():
            dd_out(i - 4, od).wait()

        cols = pl.ds(al(ft * rb, rb), rb)
        o = dot(hid[0:half, cols], wb[slot, :, 0:cq], TN)
        o += dot(hid[half:tok, cols], wb[slot, :, cq : 2 * cq], TN)
        out[ft, 0] = o.astype(BF16)

        @on_stay
        def _():
            dd_out(i, od).start()

        @on_swap
        def _():
            dd_out(i, cwd).start()

    def w_load(q, a, src):
        rows = pl.ds(al(q * cq, cq), cq)
        slot = lax.rem(q, 2)
        return pltpu.make_async_copy(
            src.at[rows, :], wb.at[0, pl.ds(al(slot * cq, cq), cq), pl.ds(a * ff, ff)], wsem.at[4 + 2 * slot + a]
        )

    def cross_w(q, l, a):
        rows = pl.ds(al(q * cq, cq), cq)
        cols = pl.ds(l * fh, fh)
        src, dst = ((wg, cwg), (wu, cwu))[a]
        j = 5 + 2 * q + a
        return remote(src.at[rows, cols], dst.at[rows, cols], csend.at[l, j], crecv.at[l, j], pdp, links[l])

    @scope("w_start")
    def w_start(q):
        @on_stay
        def _():
            for a in BOTH:
                w_load(q, a, (wg, wu)[a]).start()

        @on_swap
        def _():
            for a in BOTH:
                for l in BOTH:
                    cross_w(q, l, a).wait_recv()
                w_load(q, a, (cwg, cwu)[a]).start()

    @pl.loop(0, 16)
    def _(i):
        @pl.when(i == 12)
        def _():
            w_start(0)

        down_tile(i)
        ring_steps(DURING_DOWN, i)

    for i in range(12, 16):
        dd_out(i, od).wait()

    @on_swap
    def _():
        for l in BOTH:
            cross(l, 13).start()

    def own_f(i):
        return blk_f(i, i)

    def other_f(i):
        return stay_f(i, team) * swap + swap_f(i, team) * stay

    def xf_out(step):
        q, i, o = step // ring_len, lax.rem(step, ring_len), lax.rem(step, 2)
        rows = pl.ds(al(own_f(i) * rb, rb), rb)
        return pltpu.make_async_copy(xf.at[o], dxp.at[rows, pl.ds(al(q * cq, cq), cq)], xfs.at[o])

    def xb_out(q, i, o):
        rows = pl.ds(al(other_f(i) * rb, rb), rb)
        return remote(out.at[o, 0], dxr.at[rows, pl.ds(al(q * cq, cq), cq)], xbs.at[o], drr.at[q, i], pdp, t)

    def xb_send(step):
        return xb_out(step // ring_len, lax.rem(step, ring_len), lax.rem(step, 2))

    def rs_nbr(dn):
        return prv * (1 - dn) + nxt * dn

    def rs_send(dn, k, u, slot):
        return remote(rso.at[slot], rsl.at[dn, k, u], rss.at[slot], rsr.at[dn, k, u], dp, rs_nbr(dn))

    def slot_free(slot):
        pltpu.make_async_copy(rso.at[slot], rso.at[slot], rss.at[slot]).wait()

    def rs_part(which, slot, blk, dn, u):
        rows = pl.ds(al(blk * rb + dn * hb, hb), hb)
        cols = pl.ds(al(u * kd, kd), kd)
        src, dst = ((dxp, rpx), (dxr, rpr))[which]
        return pltpu.make_async_copy(src.at[rows, cols], dst.at[slot], rls.at[slot, which])

    def rs_sum(slot, to, received):
        @pl.loop(0, hb // 16)
        def _(i):
            rows = pl.ds(al(i * 16, 16), 16)
            v = rpx[slot, rows, :] + rpr[slot, rows, :].astype(F32)
            if received:
                v += rin[slot, rows, :].astype(F32)
            rso[to, rows, :] = v.astype(BF16)

    @scope("sum_start")
    def rs_start(u):
        for q in (2 * u, 2 * u + 1):
            for i in range(ring_len):
                own = pl.ds(al(own_f(i) * rb, rb), rb)
                remote(out.at[0, 0], dxr.at[own, pl.ds(q * cq, cq)], xbs.at[0], drr.at[q, i], pdp, t).wait_recv()

        def first(blks, k, base):
            for dn in BOTH:
                for which in BOTH:
                    rs_part(which, dn, blks[dn], dn, u).start()
            for dn in BOTH:
                for which in BOTH:
                    rs_part(which, dn, blks[dn], dn, u).wait()
                slot = base + 2 * u + dn
                rs_sum(dn, slot, False)
                rs_send(dn, k, u, slot).start()

        first((blk_f(r + 1, r + 1), blk_f(r - 1, r + 5)), 0, 0)

        @on_swap
        def _():
            first((swap_f(r - 1, team), swap_f(r - 1, team)), 5, 4)

    def rs_place(tt):
        k = tt // 4
        u = lax.rem(tt, 4) // 2
        dn = lax.rem(tt, 2)
        late = jnp.where(k == 5, 1, 0)
        q_stay = (r - 6 + k) * (1 - dn) + (r + 6 - k) * dn
        q_swap = (r - 6 + k + late) * (1 - dn) + (r + 4 - k - late) * dn
        return k, u, dn, blk_f(q_stay, q_swap)

    def rs_in(dn, k, u, slot):
        return pltpu.make_async_copy(rsl.at[dn, k, u], rin.at[slot], rls.at[slot, 2])

    @scope("sum_take")
    def rs_take(tt, slot):
        k, u, dn, blk = rs_place(tt)

        @pl.when((stay == 1) | (k < 6))
        def _():
            rs_part(0, slot, blk, dn, u).start()
            rs_part(1, slot, blk, dn, u).start()
            rs_send(dn, k, u, 0).wait_recv()
            rs_in(dn, k, u, slot).start()

    def dx_out(dn, u, slot):
        cols = pl.ds(al(u * kd, kd), kd)
        return pltpu.make_async_copy(rso.at[slot], dx.at[pl.ds(al(dn * hb, hb), hb), cols], rss.at[slot])

    def rs_back(l, dn, u, slot):
        return remote(rso.at[slot], crs.at[l, dn, u], rss.at[slot], crr.at[l, dn, u], pdp, cx * (1 - l) + cy * l)

    @scope("sum_give")
    def rs_give(tt, slot):
        k, u, dn, blk = rs_place(tt)
        to = lax.rem(tt, 8)

        @pl.when((stay == 1) | (k < 6))
        def _():
            rs_part(0, slot, blk, dn, u).wait()
            rs_part(1, slot, blk, dn, u).wait()
            rs_in(dn, k, u, slot).wait()

            @pl.when((k != 1) | (swap == 1))
            def _():
                slot_free(to)

            rs_sum(slot, to, True)

            @pl.when(k < 4 + 2 * stay)
            def _():
                rs_send(dn, k + 1, u, to).start()

            @pl.when(k == 6)
            def _():
                dx_out(dn, u, to).start()

            @pl.when((swap == 1) & (k >= 4))
            def _():
                is_r = (k - 4) * (1 - dn) + (5 - k) * dn
                rs_back(lax.rem(is_r + odd, 2), dn, u, to).start()

    @pl.loop(0, 4 * ring_len)
    @scope("dx")
    def _(step):
        q = step // ring_len
        i = lax.rem(step, ring_len)
        o = lax.rem(step, 2)

        @pl.when(step == SUMS_AT[0] * stay + SUMS_AT[1] * swap)
        def _():
            rs_start(0)

        @pl.when(i == 0)
        def _():
            for a in BOTH:
                w_load(q, a, wg).wait()

        @pl.when((i == 5) & (q < 3))
        def _():
            w_start(q + 1)

        @pl.when(step >= 2)
        def _():
            xf_out(step - 2).wait()
            xb_send(step - 2).wait_send()

        w = pl.ds(al(lax.rem(q, 2) * cq, cq), cq)
        rows = pl.ds(al(own_f(i) * rb, rb), rb)
        xf[o] = dot(dgu[rows, :], wb[0, w, :], NT)
        xf_out(step).start()
        rows = pl.ds(al(other_f(i) * rb, rb), rb)
        out[o, 0] = dot(dgu[rows, :], wb[0, w, :], NT).astype(BF16)
        xb_send(step).start()
        ring_steps(DURING_DX, step)

    for step in (4 * ring_len - 2, 4 * ring_len - 1):
        xf_out(step).wait()
        xb_send(step).wait_send()

    ring_step(1, 6)
    rs_start(1)
    for dn in BOTH:
        for i in range(8):
            for u in PIECES:
                d2d(1, dn, i, u, t).wait_recv()

    def x_cols(i):
        slot = lax.rem(i, 4)
        return pltpu.make_async_copy(
            xg.at[:, pl.ds(al(i * rb, rb), rb)], hid.at[:, pl.ds(al(slot * rb, rb), rb)], wsem.at[slot]
        )

    def dw_local(i, a):
        o = lax.rem(i, 4)
        return pltpu.make_async_copy(out.at[o, a], (og, ou)[a].at[pl.ds(al(i * rb, rb), rb), :], osem.at[o, a, 0])

    def dw_remote(i, a, l):
        o = lax.rem(i, 4)
        rows = pl.ds(al(i * rb, rb), rb)
        cols = pl.ds(l * fh, fh)
        return remote(out.at[o, a, :, cols], (og, ou)[a].at[rows, cols], osem.at[o, a, l], orecv.at[l, a, i], pdp, links[l])

    def dw_start(i, a):
        @on_stay
        def _():
            dw_local(i, a).start()

        @on_swap
        def _():
            for l in BOTH:
                dw_remote(i, a, l).start()

    @scope("dw_wait")
    def dw_wait(i, a):
        @on_stay
        def _():
            dw_local(i, a).wait()

        @on_swap
        def _():
            for l in BOTH:
                dw_remote(i, a, l).wait_send()

    for i in range(3):
        x_cols(i).start()

    @pl.loop(0, blocks)
    @scope("dw")
    def _(i):
        o = lax.rem(i, 4)

        @pl.when(i + 3 < blocks)
        def _():
            x_cols(i + 3).start()

        x_cols(i).wait()
        rs_take(i, 0)
        for a in BOTH:

            @pl.when(i >= 4)
            def _():
                dw_wait(i - 4, a)

            lhs = hid[:, pl.ds(al(o * rb, rb), rb)]
            out[o, a] = dot(lhs, dgu[:, a * ff : (a + 1) * ff], TN).astype(BF16)
            dw_start(i, a)
            if a == 0:
                rs_give(i, 0)

    @pl.loop(blocks, 28)
    def _(tt):
        rs_take(tt, 0)
        rs_give(tt, 0)

    @on_swap
    def _():
        for u in BOTH:
            for dn in BOTH:
                slot = 2 * u + dn
                for l in BOTH:
                    rs_back(l, dn, u, 0).wait_recv()
                pltpu.make_async_copy(crs.at[0, dn, u], rin.at[0], csem.at[0]).start()
                pltpu.make_async_copy(crs.at[1, dn, u], rin.at[1], csem.at[1]).start()
                pltpu.make_async_copy(crs.at[0, dn, u], rin.at[0], csem.at[0]).wait()
                pltpu.make_async_copy(crs.at[1, dn, u], rin.at[1], csem.at[1]).wait()
                slot_free(slot)

                @pl.loop(0, hb // 16)
                def _(i):
                    rows = pl.ds(al(i * 16, 16), 16)
                    rso[slot, rows, :] = (rin[0, rows, :].astype(F32) + rin[1, rows, :].astype(F32)).astype(BF16)

                dx_out(dn, u, slot).start()

    for i in range(blocks - 4, blocks):
        for a in BOTH:
            dw_wait(i, a)
    for slot in range(8):
        slot_free(slot)
    for a in BOTH:
        for dn in BOTH:
            for u in PIECES:
                for k in range(6):
                    ring(a, dn, k, u, t).wait_send()
                for k in range(8):
                    d2d(a, dn, k, u, t).wait_send()

    @on_stay
    def _():
        for a in BOTH:
            for dn in BOTH:
                for u in PIECES:
                    ring(a, dn, 6, u, t).wait_send()

    @on_swap
    def _():
        for l in BOTH:
            for j in range(14):
                cross(l, j).wait_send()
            cross(l, 13).wait_recv()

            @pl.loop(0, blocks)
            def _(j):
                for h in BOTH:
                    for a in BOTH:
                        cross_gu(l, j, h, a, t).wait_send()
                for a in BOTH:
                    dw_remote(j, a, l).wait_recv()


def copy_out(*refs):
    count = len(refs) // 4
    srcs, dsts, bufs, sems = (refs[i * count : (i + 1) * count] for i in range(4))
    moves = []
    for src, dst, buf, sem in zip(srcs, dsts, bufs, sems):
        pieces = sem.shape[1]
        rows = src.shape[0] // pieces
        for i in range(pieces):
            at = pl.ds(i * rows, rows)
            moves.append(
                (
                    pltpu.make_async_copy(src.at[at], buf.at[at], sem.at[0, i]),
                    pltpu.make_async_copy(buf.at[at], dst.at[at], sem.at[1, i]),
                )
            )
    for load, _ in moves:
        load.start()
    for load, store in moves:
        load.wait()
        store.start()
    for _, store in moves:
        store.wait()


def solution(mesh):
    side = math.isqrt(mesh.shape["tp"])

    def local(x, dy, gate, up, wg, wu, wd):
        rb, d = x.shape
        tok, ff = gate.shape
        hb, kd, blocks = rb // 2, d // 2, tok // rb

        def hbm(*shape, dtype=BF16):
            return jax.ShapeDtypeStruct(shape, dtype)

        outs = [
            hbm(rb, d), hbm(d, ff), hbm(d, ff), hbm(ff, d),
            hbm(tok, d), hbm(tok, d),
            hbm(tok, ff), hbm(tok, ff), hbm(d, ff), hbm(d, ff), hbm(ff, d),
            hbm(tok, d, dtype=F32), hbm(tok, d),
            hbm(2, 7, 2, hb, kd), hbm(2, 2, 2, hb, kd),
        ]
        sem = pltpu.SemaphoreType.DMA
        scratch = [
            pltpu.VMEM((tok, 2 * ff), BF16),
            pltpu.VMEM((tok, ff), BF16),
            pltpu.VMEM((2, tok // 2, kd), BF16),
            pltpu.VMEM((2, 2, rb, ff), BF16),
            pltpu.VMEM((4, 2, rb, ff), BF16),
            pltpu.VMEM((2, rb, d // 4), F32),
            pltpu.VMEM((2, hb, kd), BF16),
            pltpu.VMEM((2, hb, kd), F32),
            pltpu.VMEM((2, hb, kd), BF16),
            pltpu.VMEM((8, hb, kd), BF16),
            sem((2, 2, 7, SUB)), sem((2, 2, 7, SUB)), sem((2, 2, 8, SUB)), sem((2, 2, 8, SUB)),
            sem((2, 14)), sem((2, 14)), sem((2, blocks, 2, 2)), sem((2, blocks, 2, 2)),
            sem((8,)), sem((2, 2, 4)), sem((4, 2, 2)), sem((2, 2, blocks)),
            sem((2,)), sem((2,)), sem((4, 2 * side)), sem((8,)), sem((2, 7, 2)), sem((2, 3)), sem((2, 2, 2)), sem((2,)),
        ]
        res = pl.pallas_call(
            functools.partial(kernel, side),
            out_shape=outs,
            in_specs=[pl.BlockSpec(memory_space=pl.ANY)] * 7,
            out_specs=[pl.BlockSpec(memory_space=pl.ANY)] * len(outs),
            scratch_shapes=scratch,
            compiler_params=pltpu.CompilerParams(
                collective_id=0, has_side_effects=True, vmem_limit_bytes=64 * 2**20 - 2**16
            ),
            name="gated_mlp_backward",
        )(x, dy, gate, up, wg, wu, wd)
        res = res[:4]
        anywhere = [pl.BlockSpec(memory_space=pl.ANY)] * len(res)
        return pl.pallas_call(
            copy_out,
            out_shape=[hbm(*v.shape) for v in res],
            in_specs=anywhere,
            out_specs=anywhere,
            scratch_shapes=[pltpu.VMEM(v.shape, BF16) for v in res]
            + [sem((2, max(1, v.size // (4 * rb * ff)))) for v in res],
            compiler_params=pltpu.CompilerParams(vmem_limit_bytes=48 * 2**20),
            name="copy_out",
        )(*res)

    rows, cols = P(("dp", "tp"), None), P("dp", "tp")
    return jax.shard_map(
        local,
        mesh=mesh,
        in_specs=(rows, rows, cols, cols, P(None, "tp"), P(None, "tp"), P("tp", None)),
        out_specs=(rows, cols, cols, rows),
        check_vma=False,
    )
```

time: 604 us -> 498 us (0.82)
  Pallas kernels: 0 us -> 494 us
  matrix products: 289 us -> 0 us
  waiting for transfers between devices: 272 us -> 0 us
  local copies, waits for them, and re-layouts: 23.9 us -> 1.58 us
  between operations: 14 us -> 0.81 us
    pallas_call x0 -> x2, Pallas kernels: none -> 494 us  [the longest x1 477 us: local(): pl.pallas_call(functools.partial(kernel, side), out_shape=outs, in_specs=...]
    dot_general x6 -> x0, matrix products: 289 us -> none  [the longest x3 151 us: by_group(): jnp.einsum('gta,gtb->gab', a, b, preferred_element_type=jnp.float32)]
    unnamed x5 -> x0, waiting for transfers between devices: 216 us -> none
    reshape x1 -> x0, waiting for transfers between devices: 56 us -> none  [by_group(): a, b = (t.reshape(groups, -1, t.shape[-1]) for t in (a, b))]
    unnamed x2, local copies, waits for them, and re-layouts: 23.9 us -> 1.58 us
  transfers between devices with their start and end apart: 3 -> 0, of which waited for: 3 -> 0; matrix products, arithmetic and copies ran while one was open for 52% -> 0% of each run, Pallas kernels for 0% -> 0%
where the time goes in v1:
time: 498 us; the launch traced here: 497 us
  Pallas kernels  494 us (99%)
    pallas_call x1, Pallas kernels, local(): pl.pallas_call(functools.partial(kernel, side), out_shape=outs, in_specs=...  477 us
    pallas_call x1, Pallas kernels, local(): pl.pallas_call(copy_out, out_shape=[hbm(*v.shape) for v in res], in_specs...  16.9 us

profile of v1, /device:TPU:97, one launch (start us, length us, event | category | flops | bytes accessed | tf_op | source)
XLA Modules:
  0.0 496.7 jit_solution(16519694411845634713)
XLA Ops:
  0.6 477.4 %gated_mlp_backward.1 = (bf16[256,4096]{1,0:T(8,128)(2,1)}, bf16[4096,1024]{1,0:T(8,128)(2,1)}, bf16[4096,1024]{1,0:T(8,128)(2,1)}, bf16[1024,4096]{1,0:T(8,128)...) custom-call(bf16[256,4096]{1,0:T(8,128)(2,1)} %x_in.1, ...), custom_call_target="tpu_custom_call" | custom-call | tf_op jit(solution)/shard_map/gated_mlp_backward/pallas_call | solution.py:854
  478.0 0.0 copy-start
  478.0 1.6 copy-done
  479.6 16.9 %copy_out.1 = (bf16[256,4096]{1,0:T(8,128)(2,1)}, bf16[4096,1024]{1,0:T(8,128)(2,1)}, bf16[4096,1024]{1,0:T(8,128)(2,1)}, bf16[1024,4096]{1,0:T(8,128)(2,1)}) custom-call(bf16[256,4096]{1,0:T(8,128)(2,1)S(1)} %copy-done, bf16[4096,1024]{1,0:T(8,128)(2,1)} %get-tuple-element.9.refs_1_, bf16[4096,1024]{1,0:T(8,128)(2,1)} %get-tuple-element.10.refs_2_, ...), custom_call_target="tpu_custom_call" | custom-call | tf_op jit(solution)/shard_map/copy_out/pallas_call | solution.py:867
Async XLA Ops:
  478.0 1.6 copy-start

commit v2 on v1

--- a/solution.py
+++ b/solution.py
@@ -18,11 +18,15 @@
 PIECES = tuple(range(SUB))
 
 X_AFTER = 9
-X_START = (0, 6)
-DURING_CHUNKS = ((0, 2, 2, 2), (0, 3, 4, 6), (0, 4, 6, 8), (0, 5, 8, 10), (0, 6, 10, 10), (1, 0, 12, 14))
-DURING_DOWN = ((1, 1, 5, 6), (1, 2, 14, 15))
-DURING_DX = ((1, 3, 6, 7), (1, 4, 15, 16), (1, 5, 25, 26))
-SUMS_AT = (29, 18)
+START = -1
+SUMS = -2
+NEVER = -1
+DURING_CHUNKS = (
+    (0, 2, 2, 2), (0, 3, 4, 6), (0, 4, 6, 8), (0, 5, 8, 10), (0, 6, 10, NEVER),
+    (1, START, 10, 10), (1, 0, 12, 14),
+)
+DURING_DOWN = ((1, 1, 3, 5),)
+DURING_DX = ((1, 2, 5, 6), (1, 3, 14, 14), (1, 4, 23, 22), (1, 5, 31, 30), (1, SUMS, 31, 23))
 
 
 scope = jax.named_scope
@@ -37,8 +41,8 @@
     x_in, dy_in, gate, up, wg, wu, wd,
     dx, og, ou, od, xg, dyg, cg, cu, cwg, cwu, cwd, dxp, dxr, rsl, crs,
     dgu, hid, wb, gu, out, xf, rin, rpx, rpr, rso,
-    rsend, rrecv, dsend, drecv, csend, crecv, gsend, grecv,
-    wsem, lsem, osem, orecv, xfs, xbs, drr, rss, rsr, rls, crr, csem,
+    rsend, rrecv, dsend, drecv, csend, crecv, grecv,
+    wsem, lsem, osem, orecv, xfs, xbs, drr, rss, rsr, rls, crr, csem, dsem,
 ):
     n = side
     ring_len = 2 * n
@@ -147,35 +151,39 @@
     def ring(a, dn, i, u, blk, own=False):
         dst = gath[a].at[rows_of(blk, dn, u)]
         src = ins[a].at[pl.ds(dn * hb + u * piece, piece)] if own else dst
-        return remote(src, dst, rsend.at[a, dn, i, u], rrecv.at[a, dn, i, u], dp, nbr[dn])
+        return remote(src, dst, rsend.at[a], rrecv.at[a, dn, i, u], dp, nbr[dn])
 
     def d2d(a, dn, i, u, blk, own=False):
         dst = gath[a].at[rows_of(blk, dn, u)]
         src = ins[a].at[pl.ds(dn * hb + u * piece, piece)] if own else dst
-        return remote(src, dst, dsend.at[a, dn, i, u], drecv.at[a, dn, i, u], pdp, t)
+        return remote(src, dst, dsend.at[a], drecv.at[a, i], pdp, t)
+
+    def d2d_wait(a, i):
+        pltpu.make_async_copy(dyg.at[pl.ds(0, rb)], gath[a].at[pl.ds(0, rb)], drecv.at[a, i]).wait()
 
     def cross(l, j):
         cols = pl.ds(l * fh, fh)
-        if j in (0, 1, 3, 4):
-            a, h = (0, j) if j < 2 else (1, j - 3)
-            src = ins[a].at[pl.ds(h * hb, hb)]
-            dst = gath[a].at[pl.ds(al(t * rb + h * hb, hb), hb)]
-        elif j == 2:
+        if j < 2:
+            src, dst = ins[j], gath[j].at[pl.ds(al(t * rb, rb), rb)]
+        else:
             src, dst = wd.at[cols], cwd.at[cols]
-        elif j < 13:
-            q = (j - 5) // 2
-            w, cw = ((wg, cwg), (wu, cwu))[(j - 5) % 2]
-            rows = pl.ds(q * cq, cq)
-            src, dst = w.at[rows, cols], cw.at[rows, cols]
-        else:
-            src, dst = cwd.at[cols], od.at[cols]
-        return remote(src, dst, csend.at[l, j], crecv.at[l, j], pdp, links[l])
+        return remote(src, dst, csend.at[l], crecv.at[l, j], pdp, links[l])
+
+    def down_send(l, q):
+        at = (pl.ds(l * fh, fh), pl.ds(q * cq, cq))
+        return remote(cwd.at[at], od.at[at], csend.at[l], orecv.at[l], pdp, links[l])
+
+    def cross_w(q, l, a):
+        rows = pl.ds(al(q * cq, cq), cq)
+        cols = pl.ds(l * fh, fh)
+        src, dst = ((wg, cwg), (wu, cwu))[a]
+        return remote(src.at[rows, cols], dst.at[rows, cols], csend.at[l], crecv.at[l, 3 + 2 * q + a], pdp, links[l])
 
     def cross_gu(l, j, h, a, f):
         rows = pl.ds(al(f * rb + h * hb, hb), hb)
         cols = pl.ds(l * fh, fh)
         src, dst = ((gate, cg), (up, cu))[a]
-        return remote(src.at[rows, cols], dst.at[rows, cols], gsend.at[l, j, h, a], grecv.at[l, j, h, a], pdp, links[l])
+        return remote(src.at[rows, cols], dst.at[rows, cols], csend.at[l], grecv.at[j], pdp, links[l])
 
     def their_chunk(l, j):
         f = links[l]
@@ -208,8 +216,7 @@
         @on_swap
         def _():
             for l in BOTH:
-                for h in BOTH:
-                    cross(l, 3 * a + h).wait_recv()
+                cross(l, a).wait_recv()
             for i in BOTH:
                 for u in PIECES:
                     for dn in BOTH:
@@ -246,9 +253,12 @@
 
             @pl.when(i == on_stay_at * stay + on_swap_at * swap)
             def _():
-                ring_step(a, k)
-                if (a, k) == X_START:
-                    ring_start(1)
+                if k == SUMS:
+                    rs_start(0)
+                elif k == START:
+                    ring_start(a)
+                else:
+                    ring_step(a, k)
 
     def bounce(a, h, kb, out_):
         vm = dgu.at[pl.ds((2 * a + kb) * rb + h * hb, hb), :]
@@ -264,7 +274,7 @@
 
     @on_swap
     def _():
-        for j in range(3):
+        for j in (0, 2):
             for l in BOTH:
                 cross(l, j).start()
         cross_chunks(0, early)
@@ -295,13 +305,15 @@
     @on_swap
     def _():
         cross_chunks(early, X_AFTER)
-        for j in (3, 4):
-            for l in BOTH:
-                cross(l, j).start()
+        for l in BOTH:
+            cross(l, 1).start()
         cross_chunks(X_AFTER, blocks)
-        for j in range(5, 13):
-            for l in BOTH:
-                cross(l, j).start()
+
+        @pl.loop(0, 4)
+        def _(q):
+            for a in BOTH:
+                for l in BOTH:
+                    cross_w(q, l, a).start()
 
     ring_step(0, 1)
 
@@ -331,9 +343,7 @@
         @pl.when(sw != swap)
         def _():
             idx = jnp.where(j == 0, 7, jnp.where(j < 3, 5 + j, k))
-            for dn in BOTH:
-                for u in PIECES:
-                    d2d(0, dn, idx, u, halves[dn]).wait_recv()
+            d2d_wait(0, idx)
 
         for h in BOTH:
             for kb in BOTH:
@@ -347,10 +357,7 @@
 
         @on_swap
         def _():
-            for l in BOTH:
-                for h in BOTH:
-                    for a in BOTH:
-                        cross_gu(l, j, h, a, halves[h]).wait_recv()
+            pltpu.make_async_copy(dyg.at[pl.ds(0, hb)], xg.at[pl.ds(0, hb)], grecv.at[j]).wait()
             for h in BOTH:
                 for a in BOTH:
                     chunk_load(j, slot, h, 4 + a, halves[h]).start()
@@ -410,39 +417,41 @@
         )
 
     def dd_out(i, to):
-        rows = pl.ds(al(lax.rem(i, 4) * rb, rb), rb)
+        ft = lax.rem(i, 4)
+        rows = pl.ds(al(ft * rb, rb), rb)
         cols = pl.ds(al((i // 4) * cq, cq), cq)
-        o = lax.rem(i, 4)
-        return pltpu.make_async_copy(out.at[o, 0], to.at[rows, cols], osem.at[o, 0, 0])
-
-    for q in BOTH:
+        return pltpu.make_async_copy(gu.at[ft // 2, lax.rem(ft, 2)], to.at[rows, cols], dsem.at[ft])
+
+    def dd_remote(i):
+        ft = lax.rem(i, 4)
+        l = ft // 2
+        at = (pl.ds(al(ft * rb, rb), rb), pl.ds(al((i // 4) * cq, cq), cq))
+        return remote(gu.at[l, lax.rem(ft, 2)], od.at[at], dsem.at[ft], orecv.at[l], pdp, cx * (1 - l) + cy * l)
+
+    def dy_slot(q):
+        return (q + 1) // 2 % 2
+
+    def dy_start(q):
         for th in BOTH:
-            dy_cols(q, q, th).start()
+            dy_cols(q, dy_slot(q), th).start()
 
     @scope("dw_down")
-    def down_tile(i):
+    def down_tile(i, early):
         q = i // 4
         ft = lax.rem(i, 4)
-        slot = lax.rem(q, 2)
+        slot = dy_slot(q)
 
         @pl.when(ft == 0)
         def _():
             for th in BOTH:
                 dy_cols(q, slot, th).wait()
 
-            @pl.when((q == 1) | (q == 2))
-            def _():
-                for th in BOTH:
-                    dy_cols(q + 1, 1 - slot, th).start()
-
-        @pl.when(i >= 4)
-        def _():
-            dd_out(i - 4, od).wait()
-
+        if not early:
+            pl.when(i >= 12)(lambda: dd_out(i - 4, od).wait())
         cols = pl.ds(al(ft * rb, rb), rb)
         o = dot(hid[0:half, cols], wb[slot, :, 0:cq], TN)
         o += dot(hid[half:tok, cols], wb[slot, :, cq : 2 * cq], TN)
-        out[ft, 0] = o.astype(BF16)
+        gu[ft // 2, lax.rem(ft, 2)] = o.astype(BF16)
 
         @on_stay
         def _():
@@ -450,7 +459,16 @@
 
         @on_swap
         def _():
-            dd_out(i, cwd).start()
+            (dd_out(i, cwd) if early else dd_remote(i)).start()
+
+    def down_end(q):
+        for ft in range(4):
+            dd_out(4 * q + ft, od).wait()
+
+        @on_swap
+        def _():
+            for l in BOTH:
+                down_send(l, q).start()
 
     def w_load(q, a, src):
         rows = pl.ds(al(q * cq, cq), cq)
@@ -459,13 +477,6 @@
             src.at[rows, :], wb.at[0, pl.ds(al(slot * cq, cq), cq), pl.ds(a * ff, ff)], wsem.at[4 + 2 * slot + a]
         )
 
-    def cross_w(q, l, a):
-        rows = pl.ds(al(q * cq, cq), cq)
-        cols = pl.ds(l * fh, fh)
-        src, dst = ((wg, cwg), (wu, cwu))[a]
-        j = 5 + 2 * q + a
-        return remote(src.at[rows, cols], dst.at[rows, cols], csend.at[l, j], crecv.at[l, j], pdp, links[l])
-
     @scope("w_start")
     def w_start(q):
         @on_stay
@@ -480,22 +491,20 @@
                     cross_w(q, l, a).wait_recv()
                 w_load(q, a, (cwg, cwu)[a]).start()
 
-    @pl.loop(0, 16)
-    def _(i):
-        @pl.when(i == 12)
-        def _():
+    dy_start(0)
+    dy_start(1)
+
+    for q in BOTH:
+
+        @pl.loop(4 * q, 4 * q + 4)
+        def _(i):
+            down_tile(i, True)
+            ring_steps(DURING_DOWN, i)
+
+        if q:
             w_start(0)
-
-        down_tile(i)
-        ring_steps(DURING_DOWN, i)
-
-    for i in range(12, 16):
-        dd_out(i, od).wait()
-
-    @on_swap
-    def _():
-        for l in BOTH:
-            cross(l, 13).start()
+        down_end(q)
+    dy_start(2)
 
     def own_f(i):
         return blk_f(i, i)
@@ -510,7 +519,7 @@
 
     def xb_out(q, i, o):
         rows = pl.ds(al(other_f(i) * rb, rb), rb)
-        return remote(out.at[o, 0], dxr.at[rows, pl.ds(al(q * cq, cq), cq)], xbs.at[o], drr.at[q, i], pdp, t)
+        return remote(out.at[o, 0], dxr.at[rows, pl.ds(al(q * cq, cq), cq)], xbs.at[o], drr.at[q // 2], pdp, t)
 
     def xb_send(step):
         return xb_out(step // ring_len, lax.rem(step, ring_len), lax.rem(step, 2))
@@ -541,10 +550,8 @@
 
     @scope("sum_start")
     def rs_start(u):
-        for q in (2 * u, 2 * u + 1):
-            for i in range(ring_len):
-                own = pl.ds(al(own_f(i) * rb, rb), rb)
-                remote(out.at[0, 0], dxr.at[own, pl.ds(q * cq, cq)], xbs.at[0], drr.at[q, i], pdp, t).wait_recv()
+        all_of_it = pl.ds(0, ring_len * rb // 2)
+        pltpu.make_async_copy(dyg.at[all_of_it], dxr.at[all_of_it], drr.at[u]).wait()
 
         def first(blks, k, base):
             for dn in BOTH:
@@ -564,22 +571,26 @@
             first((swap_f(r - 1, team), swap_f(r - 1, team)), 5, 4)
 
     def rs_place(tt):
-        k = tt // 4
-        u = lax.rem(tt, 4) // 2
+        m = tt // 4
         dn = lax.rem(tt, 2)
+        pair = lax.rem(tt // 2, 2)
+        early = jnp.where(m < 2, swap, 0)
+        k = early * 5 * pair + (1 - early) * (m - swap)
+        u = early * m + (1 - early) * pair
+        to = 4 * (early * pair + (1 - early) * lax.rem(m, 2)) + 2 * u + dn
         late = jnp.where(k == 5, 1, 0)
         q_stay = (r - 6 + k) * (1 - dn) + (r + 6 - k) * dn
         q_swap = (r - 6 + k + late) * (1 - dn) + (r + 4 - k - late) * dn
-        return k, u, dn, blk_f(q_stay, q_swap)
+        return m, k, u, dn, blk_f(q_stay, q_swap), to
 
     def rs_in(dn, k, u, slot):
         return pltpu.make_async_copy(rsl.at[dn, k, u], rin.at[slot], rls.at[slot, 2])
 
     @scope("sum_take")
     def rs_take(tt, slot):
-        k, u, dn, blk = rs_place(tt)
-
-        @pl.when((stay == 1) | (k < 6))
+        m, k, u, dn, blk, to = rs_place(tt)
+
+        @pl.when((stay == 1) | (m < 6))
         def _():
             rs_part(0, slot, blk, dn, u).start()
             rs_part(1, slot, blk, dn, u).start()
@@ -595,16 +606,15 @@
 
     @scope("sum_give")
     def rs_give(tt, slot):
-        k, u, dn, blk = rs_place(tt)
-        to = lax.rem(tt, 8)
-
-        @pl.when((stay == 1) | (k < 6))
+        m, k, u, dn, blk, to = rs_place(tt)
+
+        @pl.when((stay == 1) | (m < 6))
         def _():
             rs_part(0, slot, blk, dn, u).wait()
             rs_part(1, slot, blk, dn, u).wait()
             rs_in(dn, k, u, slot).wait()
 
-            @pl.when((k != 1) | (swap == 1))
+            @pl.when((m != 1) | (swap == 1))
             def _():
                 slot_free(to)
 
@@ -630,16 +640,13 @@
         i = lax.rem(step, ring_len)
         o = lax.rem(step, 2)
 
-        @pl.when(step == SUMS_AT[0] * stay + SUMS_AT[1] * swap)
-        def _():
-            rs_start(0)
 
         @pl.when(i == 0)
         def _():
             for a in BOTH:
                 w_load(q, a, wg).wait()
 
-        @pl.when((i == 5) & (q < 3))
+        @pl.when((i == 7) & (q < 3))
         def _():
             w_start(q + 1)
 
@@ -663,16 +670,21 @@
 
     ring_step(1, 6)
     rs_start(1)
-    for dn in BOTH:
-        for i in range(8):
-            for u in PIECES:
-                d2d(1, dn, i, u, t).wait_recv()
-
-    def x_cols(i):
+    dy_start(3)
+    for i in range(8):
+        d2d_wait(1, i)
+
+    def x_cols(i, th):
         slot = lax.rem(i, 4)
         return pltpu.make_async_copy(
-            xg.at[:, pl.ds(al(i * rb, rb), rb)], hid.at[:, pl.ds(al(slot * rb, rb), rb)], wsem.at[slot]
+            xg.at[pl.ds(th * half, half), pl.ds(al(i * rb, rb), rb)],
+            wb.at[1, :, pl.ds(al(slot * 2 * rb + th * rb, rb), rb)],
+            wsem.at[(4, 6)[th] + lax.rem(slot, 2) + 4 * (slot // 2)],
         )
+
+    def x_start(i):
+        for th in BOTH:
+            x_cols(i, th).start()
 
     def dw_local(i, a):
         o = lax.rem(i, 4)
@@ -682,7 +694,7 @@
         o = lax.rem(i, 4)
         rows = pl.ds(al(i * rb, rb), rb)
         cols = pl.ds(l * fh, fh)
-        return remote(out.at[o, a, :, cols], (og, ou)[a].at[rows, cols], osem.at[o, a, l], orecv.at[l, a, i], pdp, links[l])
+        return remote(out.at[o, a, :, cols], (og, ou)[a].at[rows, cols], osem.at[o, a, l], orecv.at[l], pdp, links[l])
 
     def dw_start(i, a):
         @on_stay
@@ -705,8 +717,19 @@
             for l in BOTH:
                 dw_remote(i, a, l).wait_send()
 
-    for i in range(3):
-        x_cols(i).start()
+    for q in (2, 3):
+
+        @pl.loop(0, 2)
+        def _(i):
+            tt = 2 * q - 4 + i
+            rs_take(tt, 0)
+            down_tile(4 * q + 2 * i, False)
+            rs_give(tt, 0)
+            down_tile(4 * q + 2 * i + 1, False)
+
+        if q == 2:
+            for i in range(3):
+                x_start(i)
 
     @pl.loop(0, blocks)
     @scope("dw")
@@ -715,38 +738,63 @@
 
         @pl.when(i + 3 < blocks)
         def _():
-            x_cols(i + 3).start()
-
-        x_cols(i).wait()
-        rs_take(i, 0)
+            x_start(i + 3)
+
+        for th in BOTH:
+            x_cols(i, th).wait()
+        rs_take(4 + i, 0)
         for a in BOTH:
 
             @pl.when(i >= 4)
             def _():
                 dw_wait(i - 4, a)
 
-            lhs = hid[:, pl.ds(al(o * rb, rb), rb)]
-            out[o, a] = dot(lhs, dgu[:, a * ff : (a + 1) * ff], TN).astype(BF16)
+            cols = slice(a * ff, (a + 1) * ff)
+            v = dot(wb[1, :, pl.ds(al(o * 2 * rb, rb), rb)], dgu[0:half, cols], TN)
+            v += dot(wb[1, :, pl.ds(al(o * 2 * rb + rb, rb), rb)], dgu[half:tok, cols], TN)
+            out[o, a] = v.astype(BF16)
             dw_start(i, a)
             if a == 0:
-                rs_give(i, 0)
-
-    @pl.loop(blocks, 28)
+                rs_give(4 + i, 0)
+
+    @pl.loop(blocks + 4, 28)
     def _(tt):
         rs_take(tt, 0)
         rs_give(tt, 0)
 
+    def sent(sem, rows):
+        at = pl.ds(0, rows)
+        pltpu.make_async_copy(dyg.at[at], xg.at[at], sem).wait()
+
+    with scope("sent_dw"):
+        for i in range(12, 16):
+            dd_out(i, od).wait()
+        for i in range(blocks - 4, blocks):
+            for a in BOTH:
+                dw_wait(i, a)
+    for a in BOTH:
+        sent(dsend.at[a], ring_len * rb)
+        on_stay(functools.partial(sent, rsend.at[a], 14 * hb))
+        on_swap(functools.partial(sent, rsend.at[a], 12 * hb))
+
     @on_swap
+    @scope("tail")
     def _():
+        for l in BOTH:
+            sent(csend.at[l], 13 * rb)
+            sent(orecv.at[l], 6 * rb)
+
+        def back(dn, u, l):
+            return pltpu.make_async_copy(crs.at[l, dn, u], rin.at[l], csem.at[l])
+
         for u in BOTH:
             for dn in BOTH:
                 slot = 2 * u + dn
                 for l in BOTH:
                     rs_back(l, dn, u, 0).wait_recv()
-                pltpu.make_async_copy(crs.at[0, dn, u], rin.at[0], csem.at[0]).start()
-                pltpu.make_async_copy(crs.at[1, dn, u], rin.at[1], csem.at[1]).start()
-                pltpu.make_async_copy(crs.at[0, dn, u], rin.at[0], csem.at[0]).wait()
-                pltpu.make_async_copy(crs.at[1, dn, u], rin.at[1], csem.at[1]).wait()
+                    back(dn, u, l).start()
+                for l in BOTH:
+                    back(dn, u, l).wait()
                 slot_free(slot)
 
                 @pl.loop(0, hb // 16)
@@ -756,40 +804,9 @@
 
                 dx_out(dn, u, slot).start()
 
-    for i in range(blocks - 4, blocks):
-        for a in BOTH:
-            dw_wait(i, a)
-    for slot in range(8):
-        slot_free(slot)
-    for a in BOTH:
-        for dn in BOTH:
-            for u in PIECES:
-                for k in range(6):
-                    ring(a, dn, k, u, t).wait_send()
-                for k in range(8):
-                    d2d(a, dn, k, u, t).wait_send()
-
-    @on_stay
-    def _():
-        for a in BOTH:
-            for dn in BOTH:
-                for u in PIECES:
-                    ring(a, dn, 6, u, t).wait_send()
-
-    @on_swap
-    def _():
-        for l in BOTH:
-            for j in range(14):
-                cross(l, j).wait_send()
-            cross(l, 13).wait_recv()
-
-            @pl.loop(0, blocks)
-            def _(j):
-                for h in BOTH:
-                    for a in BOTH:
-                        cross_gu(l, j, h, a, t).wait_send()
-                for a in BOTH:
-                    dw_remote(j, a, l).wait_recv()
+    with scope("slots"):
+        for slot in range(8):
+            slot_free(slot)
 
 
 def copy_out(*refs):
@@ -846,10 +863,9 @@
             pltpu.VMEM((2, hb, kd), F32),
             pltpu.VMEM((2, hb, kd), BF16),
             pltpu.VMEM((8, hb, kd), BF16),
-            sem((2, 2, 7, SUB)), sem((2, 2, 7, SUB)), sem((2, 2, 8, SUB)), sem((2, 2, 8, SUB)),
-            sem((2, 14)), sem((2, 14)), sem((2, blocks, 2, 2)), sem((2, blocks, 2, 2)),
-            sem((8,)), sem((2, 2, 4)), sem((4, 2, 2)), sem((2, 2, blocks)),
-            sem((2,)), sem((2,)), sem((4, 2 * side)), sem((8,)), sem((2, 7, 2)), sem((2, 3)), sem((2, 2, 2)), sem((2,)),
+            sem((2,)), sem((2, 2, 7, SUB)), sem((2,)), sem((2, 8)), sem((2,)), sem((2, 11)), sem((blocks,)),
+            sem((12,)), sem((2, 2, 4)), sem((4, 2, 2)), sem((2,)),
+            sem((2,)), sem((2,)), sem((2,)), sem((8,)), sem((2, 7, 2)), sem((2, 3)), sem((2, 2, 2)), sem((2,)), sem((4,)),
         ]
         res = pl.pallas_call(
             functools.partial(kernel, side),

time: 498 us -> 488 us (0.980)
  Pallas kernels: 494 us -> 484 us
    pallas_call x1, Pallas kernels: 477 us -> 467 us  [local(): pl.pallas_call(functools.partial(kernel, side), out_shape=outs, in_specs=...]
where the time goes in v2:
time: 488 us; the launch traced here: 487 us
  Pallas kernels  484 us (99%)
    pallas_call x1, Pallas kernels, local(): pl.pallas_call(functools.partial(kernel, side), out_shape=outs, in_specs=...  467 us
    pallas_call x1, Pallas kernels, local(): pl.pallas_call(copy_out, out_shape=[hbm(*v.shape) for v in res], in_specs...  16.9 us

profile of v2, /device:TPU:97, one launch (start us, length us, event | category | flops | bytes accessed | tf_op | source)
XLA Modules:
  0.0 486.7 jit_solution(2655130675791617423)
XLA Ops:
  0.6 467.3 %gated_mlp_backward.1 = (bf16[256,4096]{1,0:T(8,128)(2,1)}, bf16[4096,1024]{1,0:T(8,128)(2,1)}, bf16[4096,1024]{1,0:T(8,128)(2,1)}, bf16[1024,4096]{1,0:T(8,128)...) custom-call(bf16[256,4096]{1,0:T(8,128)(2,1)} %x_in.1, ...), custom_call_target="tpu_custom_call" | custom-call | tf_op jit(solution)/shard_map/gated_mlp_backward/pallas_call | solution.py:870
  468.0 0.0 copy-start
  468.0 1.6 copy-done
  469.6 16.9 %copy_out.1 = (bf16[256,4096]{1,0:T(8,128)(2,1)}, bf16[4096,1024]{1,0:T(8,128)(2,1)}, bf16[4096,1024]{1,0:T(8,128)(2,1)}, bf16[1024,4096]{1,0:T(8,128)(2,1)}) custom-call(bf16[256,4096]{1,0:T(8,128)(2,1)S(1)} %copy-done, bf16[4096,1024]{1,0:T(8,128)(2,1)} %get-tuple-element.9.refs_1_, bf16[4096,1024]{1,0:T(8,128)(2,1)} %get-tuple-element.10.refs_2_, ...), custom_call_target="tpu_custom_call" | custom-call | tf_op jit(solution)/shard_map/copy_out/pallas_call | solution.py:883
Async XLA Ops:
  468.0 1.6 copy-start

commit v3 on v2

--- a/solution.py
+++ b/solution.py
@@ -26,10 +26,14 @@
     (1, START, 10, 10), (1, 0, 12, 14),
 )
 DURING_DOWN = ((1, 1, 3, 5),)
-DURING_DX = ((1, 2, 5, 6), (1, 3, 14, 14), (1, 4, 23, 22), (1, 5, 31, 30), (1, SUMS, 31, 23))
+DURING_DX = ((1, 2, 3, 4), (1, 3, 12, 13), (1, 4, 21, 22), (1, 5, 30, 31), (1, SUMS, 31, 23))
 
 
 scope = jax.named_scope
+
+
+def parity(v):
+    return lax.rem(v, 2)
 
 
 def dot(a, b, dims):
@@ -39,7 +43,7 @@
 def kernel(
     side,
     x_in, dy_in, gate, up, wg, wu, wd,
-    dx, og, ou, od, xg, dyg, cg, cu, cwg, cwu, cwd, dxp, dxr, rsl, crs,
+    fin0, fin1, rest, og, ou, od, xg, dyg, cg, cu, cwg, cwu, cwd, dxp, dxr, rsl, crs,
     dgu, hid, wb, gu, out, xf, rin, rpx, rpr, rso,
     rsend, rrecv, dsend, drecv, csend, crecv, grecv,
     wsem, lsem, osem, orecv, xfs, xbs, drr, rss, rsr, rls, crr, csem, dsem,
@@ -57,13 +61,13 @@
 
     t = lax.axis_index("tp")
     dp = lax.axis_index("dp")
-    c = lax.rem(dp, 2)
+    c = parity(dp)
     x = t // n
     y = lax.rem(t, n)
     s = lax.rem(x + y, n)
     team = s // 2
-    odd = lax.rem(s, 2)
-    swap = lax.rem(c + team, 2)
+    odd = parity(s)
+    swap = parity(c + team)
     stay = 1 - swap
     pdp = dp + 1 - 2 * c
 
@@ -93,13 +97,13 @@
 
     def stay_f(q, team):
         q = wr(q)
-        o = lax.rem(q, 2)
+        o = parity(q)
         bx = lax.rem((q + o) // 2, n)
         return bx * n + wrap(2 * team + o - bx)
 
     def swap_f(q, team):
         q = wr(q)
-        o = lax.rem(q, 2)
+        o = parity(q)
         bx = lax.rem((q + 3 * o) // 2, n)
         return bx * n + wrap(2 * (1 - team) + (1 - o) - bx)
 
@@ -118,7 +122,7 @@
 
     def chunk(j, team, r, t, cx, cy):
         k = jnp.maximum(j - 3, 0) // 2
-        sw = jnp.where((j == 1) | (j == 2) | ((j >= 4) & (lax.rem(j, 2) == 0)), 1, 0)
+        sw = jnp.where((j == 1) | (j == 2) | ((j >= 4) & (parity(j) == 0)), 1, 0)
         first = jnp.where(k == 0, 1, 0)
         st_a = jnp.where(j == 0, t, stay_f(r - 1 - k, team))
         st_b = jnp.where(j == 0, t, stay_f(r + 1 + k, team))
@@ -336,7 +340,7 @@
 
     @scope("chunk_start")
     def chunk_start(j):
-        slot = lax.rem(j, 2)
+        slot = parity(j)
         f_a, f_b, sw, k = chunk(j, team, r, t, cx, cy)
         halves = (f_a, f_b)
 
@@ -364,7 +368,7 @@
 
     @scope("chunk")
     def chunk_compute(j):
-        slot = lax.rem(j, 2)
+        slot = parity(j)
         f_a, f_b, _, _ = chunk(j, team, r, t, cx, cy)
         halves = (f_a, f_b)
         for h in BOTH:
@@ -416,32 +420,32 @@
             wsem.at[2 * slot + th],
         )
 
+    def down_rows(i):
+        return 2 * parity(i) + lax.rem(i, 4) // 2
+
     def dd_out(i, to):
-        ft = lax.rem(i, 4)
+        ft = down_rows(i)
         rows = pl.ds(al(ft * rb, rb), rb)
         cols = pl.ds(al((i // 4) * cq, cq), cq)
-        return pltpu.make_async_copy(gu.at[ft // 2, lax.rem(ft, 2)], to.at[rows, cols], dsem.at[ft])
+        return pltpu.make_async_copy(gu.at[ft // 2, parity(ft)], to.at[rows, cols], dsem.at[ft])
 
     def dd_remote(i):
-        ft = lax.rem(i, 4)
+        ft = down_rows(i)
         l = ft // 2
         at = (pl.ds(al(ft * rb, rb), rb), pl.ds(al((i // 4) * cq, cq), cq))
-        return remote(gu.at[l, lax.rem(ft, 2)], od.at[at], dsem.at[ft], orecv.at[l], pdp, cx * (1 - l) + cy * l)
-
-    def dy_slot(q):
-        return (q + 1) // 2 % 2
+        return remote(gu.at[l, parity(ft)], od.at[at], dsem.at[ft], orecv.at[l], pdp, cx * (1 - l) + cy * l)
 
     def dy_start(q):
         for th in BOTH:
-            dy_cols(q, dy_slot(q), th).start()
+            dy_cols(q, q % 2, th).start()
 
     @scope("dw_down")
     def down_tile(i, early):
         q = i // 4
-        ft = lax.rem(i, 4)
-        slot = dy_slot(q)
-
-        @pl.when(ft == 0)
+        ft = down_rows(i)
+        slot = parity(q)
+
+        @pl.when(lax.rem(i, 4) == 0)
         def _():
             for th in BOTH:
                 dy_cols(q, slot, th).wait()
@@ -451,7 +455,7 @@
         cols = pl.ds(al(ft * rb, rb), rb)
         o = dot(hid[0:half, cols], wb[slot, :, 0:cq], TN)
         o += dot(hid[half:tok, cols], wb[slot, :, cq : 2 * cq], TN)
-        gu[ft // 2, lax.rem(ft, 2)] = o.astype(BF16)
+        gu[ft // 2, parity(ft)] = o.astype(BF16)
 
         @on_stay
         def _():
@@ -472,9 +476,9 @@
 
     def w_load(q, a, src):
         rows = pl.ds(al(q * cq, cq), cq)
-        slot = lax.rem(q, 2)
+        slot = parity(q)
         return pltpu.make_async_copy(
-            src.at[rows, :], wb.at[0, pl.ds(al(slot * cq, cq), cq), pl.ds(a * ff, ff)], wsem.at[4 + 2 * slot + a]
+            src.at[rows, :], wb.at[1, pl.ds(al(slot * cq, cq), cq), pl.ds(a * ff, ff)], wsem.at[4 + 2 * slot + a]
         )
 
     @scope("w_start")
@@ -501,10 +505,12 @@
             down_tile(i, True)
             ring_steps(DURING_DOWN, i)
 
-        if q:
-            w_start(0)
         down_end(q)
-    dy_start(2)
+        dy_start(2) if q == 0 else w_start(0)
+
+    @pl.loop(8, 10)
+    def _(i):
+        down_tile(i, False)
 
     def own_f(i):
         return blk_f(i, i)
@@ -513,7 +519,7 @@
         return stay_f(i, team) * swap + swap_f(i, team) * stay
 
     def xf_out(step):
-        q, i, o = step // ring_len, lax.rem(step, ring_len), lax.rem(step, 2)
+        q, i, o = step // ring_len, lax.rem(step, ring_len), parity(step)
         rows = pl.ds(al(own_f(i) * rb, rb), rb)
         return pltpu.make_async_copy(xf.at[o], dxp.at[rows, pl.ds(al(q * cq, cq), cq)], xfs.at[o])
 
@@ -522,7 +528,7 @@
         return remote(out.at[o, 0], dxr.at[rows, pl.ds(al(q * cq, cq), cq)], xbs.at[o], drr.at[q // 2], pdp, t)
 
     def xb_send(step):
-        return xb_out(step // ring_len, lax.rem(step, ring_len), lax.rem(step, 2))
+        return xb_out(step // ring_len, lax.rem(step, ring_len), parity(step))
 
     def rs_nbr(dn):
         return prv * (1 - dn) + nxt * dn
@@ -572,12 +578,12 @@
 
     def rs_place(tt):
         m = tt // 4
-        dn = lax.rem(tt, 2)
-        pair = lax.rem(tt // 2, 2)
+        dn = parity(tt)
+        pair = parity(tt // 2)
         early = jnp.where(m < 2, swap, 0)
         k = early * 5 * pair + (1 - early) * (m - swap)
         u = early * m + (1 - early) * pair
-        to = 4 * (early * pair + (1 - early) * lax.rem(m, 2)) + 2 * u + dn
+        to = 4 * (early * pair + (1 - early) * parity(m)) + 2 * u + dn
         late = jnp.where(k == 5, 1, 0)
         q_stay = (r - 6 + k) * (1 - dn) + (r + 6 - k) * dn
         q_swap = (r - 6 + k + late) * (1 - dn) + (r + 4 - k - late) * dn
@@ -589,17 +595,13 @@
     @scope("sum_take")
     def rs_take(tt, slot):
         m, k, u, dn, blk, to = rs_place(tt)
-
-        @pl.when((stay == 1) | (m < 6))
-        def _():
-            rs_part(0, slot, blk, dn, u).start()
-            rs_part(1, slot, blk, dn, u).start()
-            rs_send(dn, k, u, 0).wait_recv()
-            rs_in(dn, k, u, slot).start()
-
-    def dx_out(dn, u, slot):
-        cols = pl.ds(al(u * kd, kd), kd)
-        return pltpu.make_async_copy(rso.at[slot], dx.at[pl.ds(al(dn * hb, hb), hb), cols], rss.at[slot])
+        rs_part(0, slot, blk, dn, u).start()
+        rs_part(1, slot, blk, dn, u).start()
+        rs_send(dn, k, u, 0).wait_recv()
+        rs_in(dn, k, u, slot).start()
+
+    def last_sum(dn, u, slot):
+        return pltpu.make_async_copy(rso.at[slot], (fin0, fin1)[dn].at[:, pl.ds(al(u * kd, kd), kd)], rss.at[slot])
 
     def rs_back(l, dn, u, slot):
         return remote(rso.at[slot], crs.at[l, dn, u], rss.at[slot], crr.at[l, dn, u], pdp, cx * (1 - l) + cy * l)
@@ -607,38 +609,71 @@
     @scope("sum_give")
     def rs_give(tt, slot):
         m, k, u, dn, blk, to = rs_place(tt)
-
-        @pl.when((stay == 1) | (m < 6))
-        def _():
-            rs_part(0, slot, blk, dn, u).wait()
-            rs_part(1, slot, blk, dn, u).wait()
-            rs_in(dn, k, u, slot).wait()
-
-            @pl.when((m != 1) | (swap == 1))
+        rs_part(0, slot, blk, dn, u).wait()
+        rs_part(1, slot, blk, dn, u).wait()
+        rs_in(dn, k, u, slot).wait()
+
+        @pl.when((m != 1) | (swap == 1))
+        def _():
+            slot_free(to)
+
+        rs_sum(slot, to, True)
+
+        @pl.when(k < 4 + stay)
+        def _():
+            rs_send(dn, k + 1, u, to).start()
+
+        for half_of in BOTH:
+
+            @pl.when((k == 4 + stay) & (dn == half_of))
             def _():
-                slot_free(to)
-
-            rs_sum(slot, to, True)
-
-            @pl.when(k < 4 + 2 * stay)
+                last_sum(half_of, u, to).start()
+
+        @pl.when((swap == 1) & (k == 5))
+        def _():
+            rs_back(parity(1 - dn + odd), dn, u, to).start()
+
+    def rest_put(dn, u):
+        blk = t
+
+        @on_stay
+        def _():
+            for which in BOTH:
+                rs_part(which, 1, blk, dn, u).start()
+            for which in BOTH:
+                rs_part(which, 1, blk, dn, u).wait()
+
+        @on_swap
+        def _():
+            l = parity(dn + odd)
+            rs_back(l, dn, u, 0).wait_recv()
+            back = pltpu.make_async_copy(crs.at[l, dn, u], rin.at[1], csem.at[0])
+            back.start()
+            back.wait()
+
+        @pl.loop(0, hb // 16)
+        def _(i):
+            rows = pl.ds(al(i * 16, 16), 16)
+
+            @on_stay
             def _():
-                rs_send(dn, k + 1, u, to).start()
-
-            @pl.when(k == 6)
+                rpx[1, rows, :] += rpr[1, rows, :].astype(F32)
+
+            @on_swap
             def _():
-                dx_out(dn, u, to).start()
-
-            @pl.when((swap == 1) & (k >= 4))
-            def _():
-                is_r = (k - 4) * (1 - dn) + (5 - k) * dn
-                rs_back(lax.rem(is_r + odd, 2), dn, u, to).start()
+                rpx[1, rows, :] = rin[1, rows, :].astype(F32)
+
+        at = (pl.ds(al(dn * hb, hb), hb), pl.ds(al(u * kd, kd), kd))
+        leave = pltpu.make_async_copy(rpx.at[1], rest.at[at], csem.at[1])
+        leave.start()
+        leave.wait()
 
     @pl.loop(0, 4 * ring_len)
     @scope("dx")
     def _(step):
         q = step // ring_len
         i = lax.rem(step, ring_len)
-        o = lax.rem(step, 2)
+        o = parity(step)
 
 
         @pl.when(i == 0)
@@ -655,12 +690,12 @@
             xf_out(step - 2).wait()
             xb_send(step - 2).wait_send()
 
-        w = pl.ds(al(lax.rem(q, 2) * cq, cq), cq)
+        w = pl.ds(al(parity(q) * cq, cq), cq)
         rows = pl.ds(al(own_f(i) * rb, rb), rb)
-        xf[o] = dot(dgu[rows, :], wb[0, w, :], NT)
+        xf[o] = dot(dgu[rows, :], wb[1, w, :], NT)
         xf_out(step).start()
         rows = pl.ds(al(other_f(i) * rb, rb), rb)
-        out[o, 0] = dot(dgu[rows, :], wb[0, w, :], NT).astype(BF16)
+        out[o, 0] = dot(dgu[rows, :], wb[1, w, :], NT).astype(BF16)
         xb_send(step).start()
         ring_steps(DURING_DX, step)
 
@@ -678,8 +713,8 @@
         slot = lax.rem(i, 4)
         return pltpu.make_async_copy(
             xg.at[pl.ds(th * half, half), pl.ds(al(i * rb, rb), rb)],
-            wb.at[1, :, pl.ds(al(slot * 2 * rb + th * rb, rb), rb)],
-            wsem.at[(4, 6)[th] + lax.rem(slot, 2) + 4 * (slot // 2)],
+            wb.at[0, :, pl.ds(al(slot * 2 * rb + th * rb, rb), rb)],
+            wsem.at[(4, 6)[th] + parity(slot) + 4 * (slot // 2)],
         )
 
     def x_start(i):
@@ -717,19 +752,19 @@
             for l in BOTH:
                 dw_remote(i, a, l).wait_send()
 
-    for q in (2, 3):
-
-        @pl.loop(0, 2)
+    @on_stay
+    def _():
+        @pl.loop(0, 4)
         def _(i):
-            tt = 2 * q - 4 + i
-            rs_take(tt, 0)
-            down_tile(4 * q + 2 * i, False)
-            rs_give(tt, 0)
-            down_tile(4 * q + 2 * i + 1, False)
-
-        if q == 2:
-            for i in range(3):
-                x_start(i)
+            rest_put(parity(i), i // 2)
+
+    @pl.loop(0, 3)
+    def _(tt):
+        rs_take(tt, 0)
+        down_tile(10 + 2 * tt, False)
+        rs_give(tt, 0)
+        down_tile(11 + 2 * tt, False)
+        x_start(tt)
 
     @pl.loop(0, blocks)
     @scope("dw")
@@ -742,7 +777,7 @@
 
         for th in BOTH:
             x_cols(i, th).wait()
-        rs_take(4 + i, 0)
+        rs_take(3 + i, 0)
         for a in BOTH:
 
             @pl.when(i >= 4)
@@ -750,15 +785,21 @@
                 dw_wait(i - 4, a)
 
             cols = slice(a * ff, (a + 1) * ff)
-            v = dot(wb[1, :, pl.ds(al(o * 2 * rb, rb), rb)], dgu[0:half, cols], TN)
-            v += dot(wb[1, :, pl.ds(al(o * 2 * rb + rb, rb), rb)], dgu[half:tok, cols], TN)
+            v = dot(wb[0, :, pl.ds(al(o * 2 * rb, rb), rb)], dgu[0:half, cols], TN)
+            v += dot(wb[0, :, pl.ds(al(o * 2 * rb + rb, rb), rb)], dgu[half:tok, cols], TN)
             out[o, a] = v.astype(BF16)
             dw_start(i, a)
             if a == 0:
-                rs_give(4 + i, 0)
-
-    @pl.loop(blocks + 4, 28)
+                rs_give(3 + i, 0)
+
+    first, last = blocks + 3, 24
+
+    @pl.loop(first, last)
     def _(tt):
+        @pl.when((swap == 1) & (tt + 1 < last))
+        def _():
+            rest_put(parity(tt - first), (tt - first) // 2)
+
         rs_take(tt, 0)
         rs_give(tt, 0)
 
@@ -784,29 +825,28 @@
             sent(csend.at[l], 13 * rb)
             sent(orecv.at[l], 6 * rb)
 
-        def back(dn, u, l):
-            return pltpu.make_async_copy(crs.at[l, dn, u], rin.at[l], csem.at[l])
-
-        for u in BOTH:
-            for dn in BOTH:
-                slot = 2 * u + dn
-                for l in BOTH:
-                    rs_back(l, dn, u, 0).wait_recv()
-                    back(dn, u, l).start()
-                for l in BOTH:
-                    back(dn, u, l).wait()
-                slot_free(slot)
-
-                @pl.loop(0, hb // 16)
-                def _(i):
-                    rows = pl.ds(al(i * 16, 16), 16)
-                    rso[slot, rows, :] = (rin[0, rows, :].astype(F32) + rin[1, rows, :].astype(F32)).astype(BF16)
-
-                dx_out(dn, u, slot).start()
-
     with scope("slots"):
         for slot in range(8):
             slot_free(slot)
+
+
+def last_hops(groups, n):
+    ways = ([], [])
+    for dp in range(groups):
+        for t in range(n * n):
+            x, y = divmod(t, n)
+            team, odd = divmod((x + y) % n, 2)
+            swap = (dp + team) % 2
+            sg = odd if swap else 1 - odd
+            step = 2 * sg - 1
+            across, along = ((x + step) % n) * n + y, x * n + (y + step) % n
+            to = (along, across) if odd else (across, along)
+            if not swap:
+                to = to[::-1]
+            to_dp = dp + 1 - 2 * (dp % 2) if swap else dp
+            for way, f in zip(ways, to):
+                way.append((dp * n * n + t, to_dp * n * n + f))
+    return ways
 
 
 def copy_out(*refs):
@@ -835,6 +875,7 @@
 
 def solution(mesh):
     side = math.isqrt(mesh.shape["tp"])
+    ways = last_hops(mesh.shape["dp"], side)
 
     def local(x, dy, gate, up, wg, wu, wd):
         rb, d = x.shape
@@ -845,11 +886,12 @@
             return jax.ShapeDtypeStruct(shape, dtype)
 
         outs = [
-            hbm(rb, d), hbm(d, ff), hbm(d, ff), hbm(ff, d),
+            hbm(hb, d), hbm(hb, d), hbm(rb, d, dtype=F32),
+            hbm(d, ff), hbm(d, ff), hbm(ff, d),
             hbm(tok, d), hbm(tok, d),
             hbm(tok, ff), hbm(tok, ff), hbm(d, ff), hbm(d, ff), hbm(ff, d),
             hbm(tok, d, dtype=F32), hbm(tok, d),
-            hbm(2, 7, 2, hb, kd), hbm(2, 2, 2, hb, kd),
+            hbm(2, 6, 2, hb, kd), hbm(2, 2, 2, hb, kd),
         ]
         sem = pltpu.SemaphoreType.DMA
         scratch = [
@@ -865,7 +907,7 @@
             pltpu.VMEM((8, hb, kd), BF16),
             sem((2,)), sem((2, 2, 7, SUB)), sem((2,)), sem((2, 8)), sem((2,)), sem((2, 11)), sem((blocks,)),
             sem((12,)), sem((2, 2, 4)), sem((4, 2, 2)), sem((2,)),
-            sem((2,)), sem((2,)), sem((2,)), sem((8,)), sem((2, 7, 2)), sem((2, 3)), sem((2, 2, 2)), sem((2,)), sem((4,)),
+            sem((2,)), sem((2,)), sem((2,)), sem((8,)), sem((2, 6, 2)), sem((2, 3)), sem((2, 2, 2)), sem((2,)), sem((4,)),
         ]
         res = pl.pallas_call(
             functools.partial(kernel, side),
@@ -878,9 +920,10 @@
             ),
             name="gated_mlp_backward",
         )(x, dy, gate, up, wg, wu, wd)
-        res = res[:4]
+        fins, rest, res = res[:2], res[2], res[3:6]
+        moved = [lax.ppermute(v, ("dp", "tp"), way) for v, way in zip(fins, ways)]
         anywhere = [pl.BlockSpec(memory_space=pl.ANY)] * len(res)
-        return pl.pallas_call(
+        grads = pl.pallas_call(
             copy_out,
             out_shape=[hbm(*v.shape) for v in res],
             in_specs=anywhere,
@@ -888,8 +931,11 @@
             scratch_shapes=[pltpu.VMEM(v.shape, BF16) for v in res]
             + [sem((2, max(1, v.size // (4 * rb * ff)))) for v in res],
             compiler_params=pltpu.CompilerParams(vmem_limit_bytes=48 * 2**20),
+            cost_estimate=pl.CostEstimate(flops=10**10, bytes_accessed=6 * d * ff * 2, transcendentals=0),
             name="copy_out",
         )(*res)
+        dx = (jnp.concatenate(moved).astype(F32) + rest).astype(BF16)
+        return dx, *grads
 
     rows, cols = P(("dp", "tp"), None), P("dp", "tp")
     return jax.shard_map(

time: 488 us -> 469 us (0.961)
  Pallas kernels: 484 us -> 459 us
    pallas_call x1, Pallas kernels: 467 us -> 442 us  [local(): pl.pallas_call(functools.partial(kernel, side), out_shape=outs, in_specs=...]
  transfers between devices with their start and end apart: 0 -> 2, of which waited for: 0 -> 0; matrix products, arithmetic and copies ran while one was open for 0% -> 0% of each run, Pallas kernels for 0% -> 4%
where the time goes in v3:
time: 469 us; the launch traced here: 465 us
  Pallas kernels  459 us (98%)
    pallas_call x1, Pallas kernels, local(): pl.pallas_call(functools.partial(kernel, side), out_shape=outs, in_specs=...  442 us
    pallas_call x1, Pallas kernels, local(): pl.pallas_call(copy_out, out_shape=[hbm(*v.shape) for v in res], in_specs...  17.1 us
  transfers between devices with their start and end apart: 2, of which 0 were waited for; matrix products, arithmetic and copies ran while one was open for 0% of the time, Pallas kernels for 4%

profile of v3, /device:TPU:97, one launch (start us, length us, event | category | flops | bytes accessed | tf_op | source)
XLA Modules:
  0.0 465.4 jit_solution(3692321823076631772)
XLA Ops:
  0.6 442.1 %gated_mlp_backward.1 = (bf16[128,4096]{1,0:T(8,128)(2,1)}, bf16[128,4096]{1,0:T(8,128)(2,1)}, f32[256,4096]{1,0:T(8,128)}, bf16[4096,1024]{1,0:T(8,128)(2,1)}, ...) custom-call(bf16[256,4096]{1,0:T(8,128)(2,1)} %x_in.1, ...), custom_call_target="tpu_custom_call" | custom-call | tf_op jit(solution)/shard_map/gated_mlp_backward/pallas_call | solution.py:912
  442.7 3.6 collective-permute-start
  446.4 0.0 collective-permute-start.1
  446.4 0.0 copy-start
  446.4 17.1 %copy_out.1 = (bf16[4096,1024]{1,0:T(8,128)(2,1)}, bf16[4096,1024]{1,0:T(8,128)(2,1)}, bf16[1024,4096]{1,0:T(8,128)(2,1)}) custom-call(bf16[4096,1024]{1,0:T(8,128)(2,1)} %get-tuple-element.16.refs_0_, bf16[4096,1024]{1,0:T(8,128)(2,1)} %get-tuple-element.17.refs_1_, bf16[1024,4096]{1,0:T(8,128)(2,1)} %get-tuple-element.18.refs_2_), custom_call_target="tpu_custom_call" | custom-call | flops 10000000000 | bytes 50331648 | tf_op jit(solution)/shard_map/copy_out/pallas_call | solution.py:926
  463.4 0.0 collective-permute-done
  463.5 0.0 collective-permute-done.1
  463.5 0.0 copy-done
  463.5 1.9 add_convert_fusion
Async XLA Ops:
  442.7 20.7 %collective-permute-start = (bf16[128,4096]{1,0:T(8,128)(2,1)}, bf16[128,4096]{1,0:T(8,128)(2,1)S(1)}, u32[]{:S(2)}, u32[]{:S(2)}) collective-permute-start(bf16[128,4096]{1,0:T(8,128)(2,1)} %get-tuple-element.13), channel_id=1, source_target_pairs={{0,1},{1,13},{2,30},{3,16},{4,0},{5,17},{6,23},{7,4},{8,20},{9,26}... | collective-permute-start | bytes 3145736 | tf_op jit(solution)/shard_map/ppermute | solution.py:924
  446.4 17.1 %collective-permute-start.1 = (bf16[128,4096]{1,0:T(8,128)(2,1)}, bf16[128,4096]{1,0:T(8,128)(2,1)S(1)}, u32[]{:S(2)}, u32[]{:S(2)}) collective-permute-start(bf16[128,4096]{1,0:T(8,128)(2,1)} %get-tuple-element.14), channel_id=1, source_target_pairs={{0,4},{1,0},{2,17},{3,23},{4,7},{5,20},{6,26},{7,11},{8,27},{9,29}... | collective-permute-start | bytes 3145736 | tf_op jit(solution)/shard_map/ppermute | solution.py:924
  446.4 17.1 %copy-start = (f32[256,4096]{1,0:T(8,128)S(1)}, f32[256,4096]{1,0:T(8,128)}, u32[]{:S(2)}) copy-start(f32[256,4096]{1,0:T(8,128)} %get-tuple-element.15) | copy-start | bytes 12582916

commit v4 on v3

--- a/solution.py
+++ b/solution.py
@@ -14,19 +14,21 @@
 NT = (((1,), (1,)), ((), ()))
 TN = (((0,), (0,)), ((), ()))
 BOTH = (0, 1)
+LATE = (2, 3)
+FOUR = range(4)
 SUB = 2
 PIECES = tuple(range(SUB))
 
 X_AFTER = 9
-START = -1
-SUMS = -2
 NEVER = -1
-DURING_CHUNKS = (
-    (0, 2, 2, 2), (0, 3, 4, 6), (0, 4, 6, 8), (0, 5, 8, 10), (0, 6, 10, NEVER),
-    (1, START, 10, 10), (1, 0, 12, 14),
+DOWN, TERMS, DONE = 16, 24, 56
+DY_AT = ((2, 4, 6, 8, 10), (2, 6, 8, 10, NEVER))
+X_START = (10, 10)
+X_AT = (
+    (12, 12, 16, 18, 23, 27, 32, 36, 41, 45, 50, 55),
+    (13, 15, 18, 21, 25, 30, 34, 38, 43, 48, 52, 55),
 )
-DURING_DOWN = ((1, 1, 3, 5),)
-DURING_DX = ((1, 2, 3, 4), (1, 3, 12, 13), (1, 4, 21, 22), (1, 5, 30, 31), (1, SUMS, 31, 23))
+SUMS_AT = (55, 49)
 
 
 scope = jax.named_scope
@@ -43,10 +45,10 @@
 def kernel(
     side,
     x_in, dy_in, gate, up, wg, wu, wd,
-    fin0, fin1, rest, og, ou, od, xg, dyg, cg, cu, cwg, cwu, cwd, dxp, dxr, rsl, crs,
-    dgu, hid, wb, gu, out, xf, rin, rpx, rpr, rso,
+    fin0, fin1, rest, short, og, ou, od, xg, dyg, cg, cu, cwg, cwu, cwd, dxp, dxr, rsl, hidr,
+    dgu, hid, wb, gu, out, xf, rin, rpx, rpr, rso, hv,
     rsend, rrecv, dsend, drecv, csend, crecv, grecv,
-    wsem, lsem, osem, orecv, xfs, xbs, drr, rss, rsr, rls, crr, csem, dsem,
+    wsem, lsem, osem, orecv, xfs, xbs, drr, rss, rsr, rls, crr, csem, dsem, hsem,
 ):
     n = side
     ring_len = 2 * n
@@ -135,7 +137,7 @@
         return pl.multiple_of(v, m)
 
     bar = pltpu.get_barrier_semaphore()
-    peers = ((dp, nxt), (dp, prv), (pdp, t), (pdp, cx), (pdp, cy))
+    peers = ((dp, nxt), (dp, prv), (pdp, t), (pdp, cx), (pdp, cy), (dp, cx), (dp, cy))
     for p, f in peers:
         pl.semaphore_signal(bar, inc=1, device_id={"dp": p, "tp": f}, device_id_type=MESH)
     pl.semaphore_wait(bar, len(peers))
@@ -230,9 +232,9 @@
                     for dn in BOTH:
                         d2d(a, dn, 6 + l, u, links[l]).start()
 
-    def ring_step(a, k):
+    def ring_step(a, k, pieces=PIECES):
         def body():
-            for u in PIECES:
+            for u in pieces:
                 for dn in BOTH:
                     b = arr_blk(dn, k)
                     ring(a, dn, k, u, b).wait_recv()
@@ -252,17 +254,18 @@
             else:
                 body()
 
-    def ring_steps(table, i):
-        for a, k, on_stay_at, on_swap_at in table:
-
-            @pl.when(i == on_stay_at * stay + on_swap_at * swap)
-            def _():
-                if k == SUMS:
-                    rs_start(0)
-                elif k == START:
-                    ring_start(a)
-                else:
-                    ring_step(a, k)
+    def ring_steps(start, end, i):
+        def at(places, act):
+            if any(start <= place < end for place in places):
+                pl.when(start + i == places[0] * stay + places[1] * swap)(act)
+
+        for k, places in enumerate(zip(*DY_AT)):
+            at(places, functools.partial(ring_step, 0, 2 + k))
+        at(X_START, lambda: ring_start(1))
+        for k, places in enumerate(zip(*X_AT)):
+            at(places, functools.partial(ring_step, 1, k // SUB, (k % SUB,)))
+        at(SUMS_AT, lambda: rs_start(0))
+        at(SUMS_AT, lambda: rs_short(0))
 
     def bounce(a, h, kb, out_):
         vm = dgu.at[pl.ds((2 * a + kb) * rb + h * hb, hb), :]
@@ -372,7 +375,7 @@
         f_a, f_b, _, _ = chunk(j, team, r, t, cx, cy)
         halves = (f_a, f_b)
         for h in BOTH:
-            for what in range(4):
+            for what in FOUR:
                 chunk_load(j, slot, h, what, halves[h]).wait()
         for nt in BOTH:
             cols = pl.ds(nt * fh, fh)
@@ -405,7 +408,7 @@
     @pl.loop(0, blocks)
     def _(j):
         chunk_compute(j)
-        ring_steps(DURING_CHUNKS, j)
+        ring_steps(0, DOWN, j)
 
         @pl.when(j + 1 + stay < blocks)
         def _():
@@ -420,59 +423,50 @@
             wsem.at[2 * slot + th],
         )
 
-    def down_rows(i):
-        return 2 * parity(i) + lax.rem(i, 4) // 2
-
-    def dd_out(i, to):
-        ft = down_rows(i)
-        rows = pl.ds(al(ft * rb, rb), rb)
-        cols = pl.ds(al((i // 4) * cq, cq), cq)
-        return pltpu.make_async_copy(gu.at[ft // 2, parity(ft)], to.at[rows, cols], dsem.at[ft])
-
-    def dd_remote(i):
-        ft = down_rows(i)
-        l = ft // 2
-        at = (pl.ds(al(ft * rb, rb), rb), pl.ds(al((i // 4) * cq, cq), cq))
-        return remote(gu.at[l, parity(ft)], od.at[at], dsem.at[ft], orecv.at[l], pdp, cx * (1 - l) + cy * l)
+    def down_at(q, ft):
+        return pl.ds(al(ft * rb, rb), rb), pl.ds(al(q * cq, cq), cq)
+
+    def down_buf(place):
+        return gu.at[place // 2, parity(place)]
+
+    def down_out(q, ft, to):
+        return pltpu.make_async_copy(down_buf(ft), to.at[down_at(q, ft)], dsem.at[ft])
+
+    def towards(l):
+        return cx * (1 - l) + cy * l
+
+    def down_remote(q, l):
+        place = 2 * l + q % 2
+        return remote(down_buf(place), od.at[down_at(q, 2 * l)], dsem.at[place], orecv.at[l], pdp, towards(l))
+
+    def help_slot(q, l):
+        return 2 * (q - 2) + l
+
+    def help_remote(q, l):
+        place = help_slot(q, l)
+        return remote(out.at[place, 0], od.at[down_at(q, 2 * l + 1)], hsem.at[4 + place], orecv.at[l], dp, towards(l))
+
+    def hidden_over(l):
+        return remote(hid.at[:, pl.ds((2 * l + 1) * rb, rb)], hidr.at[:, pl.ds(l * rb, rb)], hsem.at[0], hsem.at[1], pdp, t)
+
+    def hidden_in(sem):
+        return pltpu.make_async_copy(hidr, hv, hsem.at[sem])
 
     def dy_start(q):
         for th in BOTH:
             dy_cols(q, q % 2, th).start()
 
     @scope("dw_down")
-    def down_tile(i, early):
-        q = i // 4
-        ft = down_rows(i)
-        slot = parity(q)
-
-        @pl.when(lax.rem(i, 4) == 0)
-        def _():
-            for th in BOTH:
-                dy_cols(q, slot, th).wait()
-
-        if not early:
-            pl.when(i >= 12)(lambda: dd_out(i - 4, od).wait())
+    def down_dot(q, lhs, ft):
+        slot = q % 2
         cols = pl.ds(al(ft * rb, rb), rb)
-        o = dot(hid[0:half, cols], wb[slot, :, 0:cq], TN)
-        o += dot(hid[half:tok, cols], wb[slot, :, cq : 2 * cq], TN)
-        gu[ft // 2, parity(ft)] = o.astype(BF16)
-
-        @on_stay
-        def _():
-            dd_out(i, od).start()
-
-        @on_swap
-        def _():
-            (dd_out(i, cwd) if early else dd_remote(i)).start()
-
-    def down_end(q):
-        for ft in range(4):
-            dd_out(4 * q + ft, od).wait()
-
-        @on_swap
-        def _():
-            for l in BOTH:
-                down_send(l, q).start()
+        o = dot(lhs[0:half, cols], wb[slot, :, 0:cq], TN)
+        o += dot(lhs[half:tok, cols], wb[slot, :, cq : 2 * cq], TN)
+        return o.astype(BF16)
+
+    def dy_wait(q):
+        for th in BOTH:
+            dy_cols(q, q % 2, th).wait()
 
     def w_load(q, a, src):
         rows = pl.ds(al(q * cq, cq), cq)
@@ -495,22 +489,38 @@
                     cross_w(q, l, a).wait_recv()
                 w_load(q, a, (cwg, cwu)[a]).start()
 
+    @on_swap
+    def _():
+        for l in BOTH:
+            hidden_over(l).start()
+
     dy_start(0)
-    dy_start(1)
-
     for q in BOTH:
-
-        @pl.loop(4 * q, 4 * q + 4)
+        dy_wait(q)
+
+        @pl.loop(0, 4)
         def _(i):
-            down_tile(i, True)
-            ring_steps(DURING_DOWN, i)
-
-        down_end(q)
+            ft = 2 * parity(i) + i // 2
+            gu[ft // 2, parity(ft)] = down_dot(q, hid, ft)
+            on_stay(lambda: down_out(q, ft, od).start())
+            on_swap(lambda: down_out(q, ft, cwd).start())
+            if q == 0:
+                pl.when(i == 0)(lambda: dy_start(1))
+            ring_steps(DOWN + 4 * q, DOWN + 4 * q + 4, i)
+
+        for ft in FOUR:
+            down_out(q, ft, od).wait()
         dy_start(2) if q == 0 else w_start(0)
 
-    @pl.loop(8, 10)
-    def _(i):
-        down_tile(i, False)
+        @on_swap
+        def _():
+            for l in BOTH:
+                down_send(l, q).start()
+
+    @on_stay
+    def _():
+        hidden_in(1).wait()
+        hidden_in(2).start()
 
     def own_f(i):
         return blk_f(i, i)
@@ -554,27 +564,28 @@
                 v += rin[slot, rows, :].astype(F32)
             rso[to, rows, :] = v.astype(BF16)
 
+    def rs_first(u, blks, k, base):
+        for dn in BOTH:
+            for which in BOTH:
+                rs_part(which, dn, blks[dn], dn, u).start()
+        for dn in BOTH:
+            for which in BOTH:
+                rs_part(which, dn, blks[dn], dn, u).wait()
+            slot = base + 2 * u + dn
+            rs_sum(dn, slot, False)
+            rs_send(dn, k, u, slot).start()
+
     @scope("sum_start")
     def rs_start(u):
         all_of_it = pl.ds(0, ring_len * rb // 2)
         pltpu.make_async_copy(dyg.at[all_of_it], dxr.at[all_of_it], drr.at[u]).wait()
-
-        def first(blks, k, base):
-            for dn in BOTH:
-                for which in BOTH:
-                    rs_part(which, dn, blks[dn], dn, u).start()
-            for dn in BOTH:
-                for which in BOTH:
-                    rs_part(which, dn, blks[dn], dn, u).wait()
-                slot = base + 2 * u + dn
-                rs_sum(dn, slot, False)
-                rs_send(dn, k, u, slot).start()
-
-        first((blk_f(r + 1, r + 1), blk_f(r - 1, r + 5)), 0, 0)
-
+        rs_first(u, (blk_f(r + 1, r + 1), blk_f(r - 1, r + 5)), 0, 0)
+
+    def rs_short(u):
         @on_swap
-        def _():
-            first((swap_f(r - 1, team), swap_f(r - 1, team)), 5, 4)
+        @scope("sum_short")
+        def _():
+            rs_first(u, [swap_f(r - 1, team)] * 2, 5, 4)
 
     def rs_place(tt):
         m = tt // 4
@@ -604,7 +615,8 @@
         return pltpu.make_async_copy(rso.at[slot], (fin0, fin1)[dn].at[:, pl.ds(al(u * kd, kd), kd)], rss.at[slot])
 
     def rs_back(l, dn, u, slot):
-        return remote(rso.at[slot], crs.at[l, dn, u], rss.at[slot], crr.at[l, dn, u], pdp, cx * (1 - l) + cy * l)
+        at = (pl.ds(al(dn * hb, hb), hb), pl.ds(al(u * kd, kd), kd))
+        return remote(rso.at[slot], short.at[at], rss.at[slot], crr.at[dn, u], pdp, towards(l))
 
     @scope("sum_give")
     def rs_give(tt, slot):
@@ -634,34 +646,15 @@
             rs_back(parity(1 - dn + odd), dn, u, to).start()
 
     def rest_put(dn, u):
-        blk = t
-
-        @on_stay
-        def _():
-            for which in BOTH:
-                rs_part(which, 1, blk, dn, u).start()
-            for which in BOTH:
-                rs_part(which, 1, blk, dn, u).wait()
-
-        @on_swap
-        def _():
-            l = parity(dn + odd)
-            rs_back(l, dn, u, 0).wait_recv()
-            back = pltpu.make_async_copy(crs.at[l, dn, u], rin.at[1], csem.at[0])
-            back.start()
-            back.wait()
+        for which in BOTH:
+            rs_part(which, 1, t, dn, u).start()
+        for which in BOTH:
+            rs_part(which, 1, t, dn, u).wait()
 
         @pl.loop(0, hb // 16)
         def _(i):
             rows = pl.ds(al(i * 16, 16), 16)
-
-            @on_stay
-            def _():
-                rpx[1, rows, :] += rpr[1, rows, :].astype(F32)
-
-            @on_swap
-            def _():
-                rpx[1, rows, :] = rin[1, rows, :].astype(F32)
+            rpx[1, rows, :] += rpr[1, rows, :].astype(F32)
 
         at = (pl.ds(al(dn * hb, hb), hb), pl.ds(al(u * kd, kd), kd))
         leave = pltpu.make_async_copy(rpx.at[1], rest.at[at], csem.at[1])
@@ -691,21 +684,71 @@
             xb_send(step - 2).wait_send()
 
         w = pl.ds(al(parity(q) * cq, cq), cq)
-        rows = pl.ds(al(own_f(i) * rb, rb), rb)
-        xf[o] = dot(dgu[rows, :], wb[1, w, :], NT)
+        v = dot(jnp.concatenate([dgu[pl.ds(al(f(i) * rb, rb), rb), :] for f in (own_f, other_f)]), wb[1, w, :], NT)
+        xf[o] = v[:rb]
         xf_out(step).start()
-        rows = pl.ds(al(other_f(i) * rb, rb), rb)
-        out[o, 0] = dot(dgu[rows, :], wb[1, w, :], NT).astype(BF16)
+        out[o, 0] = v[rb:].astype(BF16)
         xb_send(step).start()
-        ring_steps(DURING_DX, step)
+        ring_steps(TERMS, DONE, step)
 
     for step in (4 * ring_len - 2, 4 * ring_len - 1):
         xf_out(step).wait()
         xb_send(step).wait_send()
 
-    ring_step(1, 6)
+    dy_start(3)
+
+    def down_put(q, ft, place):
+        gu[place // 2, parity(place)] = down_dot(q, hid, ft)
+
+    @on_stay
+    def _():
+        hidden_in(2).wait()
+        for q in LATE:
+            dy_wait(q)
+
+            @pl.loop(0, 2)
+            def _(i):
+                out[help_slot(q, i), 0] = down_dot(q, hv, i)
+                help_remote(q, i).start()
+                if q == 2:
+                    for ft in (i, 2 + i):
+                        down_put(q, ft, ft)
+                        down_out(q, ft, od).start()
+
+            ring_step(1, 6, (q - 2,))
+
     rs_start(1)
-    dy_start(3)
+    rs_short(1)
+    pl.when(swap == 1)(lambda: dy_wait(2))
+    for half_of in BOTH:
+        q = 2 + half_of
+        if half_of:
+
+            @on_stay
+            def _():
+                for dn in BOTH:
+                    rest_put(dn, 0)
+
+            pl.when(swap == 1)(lambda: dy_wait(q))
+
+        @pl.loop(0, 2)
+        def _(i):
+            tt = 2 * half_of + i
+            rs_take(tt, 0)
+
+            @on_stay
+            def _():
+                down_out(2, tt, od).wait()
+                down_put(3, tt, tt)
+                down_out(3, tt, od).start()
+
+            @on_swap
+            def _():
+                down_put(q, 2 * i, 2 * i + half_of)
+                down_remote(q, i).start()
+
+            rs_give(tt, 0)
+
     for i in range(8):
         d2d_wait(1, i)
 
@@ -752,19 +795,14 @@
             for l in BOTH:
                 dw_remote(i, a, l).wait_send()
 
+    for i in range(3):
+        x_start(i)
+
     @on_stay
     def _():
-        @pl.loop(0, 4)
-        def _(i):
-            rest_put(parity(i), i // 2)
-
-    @pl.loop(0, 3)
-    def _(tt):
-        rs_take(tt, 0)
-        down_tile(10 + 2 * tt, False)
-        rs_give(tt, 0)
-        down_tile(11 + 2 * tt, False)
-        x_start(tt)
+        for q in LATE:
+            for i in BOTH:
+                help_remote(q, i).wait_send()
 
     @pl.loop(0, blocks)
     @scope("dw")
@@ -777,7 +815,7 @@
 
         for th in BOTH:
             x_cols(i, th).wait()
-        rs_take(3 + i, 0)
+        rs_take(4 + i, 0)
         for a in BOTH:
 
             @pl.when(i >= 4)
@@ -790,16 +828,11 @@
             out[o, a] = v.astype(BF16)
             dw_start(i, a)
             if a == 0:
-                rs_give(3 + i, 0)
-
-    first, last = blocks + 3, 24
-
-    @pl.loop(first, last)
+                rs_give(4 + i, 0)
+
+    @pl.loop(blocks + 4, 24)
     def _(tt):
-        @pl.when((swap == 1) & (tt + 1 < last))
-        def _():
-            rest_put(parity(tt - first), (tt - first) // 2)
-
+        pl.when((stay == 1) & (tt < blocks + 6))(lambda: rest_put(parity(tt), 1))
         rs_take(tt, 0)
         rs_give(tt, 0)
 
@@ -808,8 +841,10 @@
         pltpu.make_async_copy(dyg.at[at], xg.at[at], sem).wait()
 
     with scope("sent_dw"):
-        for i in range(12, 16):
-            dd_out(i, od).wait()
+        for ft in FOUR:
+            down_out(3, ft, od).wait()
+
+        on_swap(lambda: hidden_in(0).wait())
         for i in range(blocks - 4, blocks):
             for a in BOTH:
                 dw_wait(i, a)
@@ -824,6 +859,9 @@
         for l in BOTH:
             sent(csend.at[l], 13 * rb)
             sent(orecv.at[l], 6 * rb)
+        for dn in BOTH:
+            for u in BOTH:
+                rs_back(0, dn, u, 0).wait_recv()
 
     with scope("slots"):
         for slot in range(8):
@@ -851,7 +889,7 @@
 
 def copy_out(*refs):
     count = len(refs) // 4
-    srcs, dsts, bufs, sems = (refs[i * count : (i + 1) * count] for i in range(4))
+    srcs, dsts, bufs, sems = (refs[i * count : (i + 1) * count] for i in FOUR)
     moves = []
     for src, dst, buf, sem in zip(srcs, dsts, bufs, sems):
         pieces = sem.shape[1]
@@ -886,12 +924,12 @@
             return jax.ShapeDtypeStruct(shape, dtype)
 
         outs = [
-            hbm(hb, d), hbm(hb, d), hbm(rb, d, dtype=F32),
+            hbm(hb, d), hbm(hb, d), hbm(rb, d, dtype=F32), hbm(rb, d),
             hbm(d, ff), hbm(d, ff), hbm(ff, d),
             hbm(tok, d), hbm(tok, d),
             hbm(tok, ff), hbm(tok, ff), hbm(d, ff), hbm(d, ff), hbm(ff, d),
             hbm(tok, d, dtype=F32), hbm(tok, d),
-            hbm(2, 6, 2, hb, kd), hbm(2, 2, 2, hb, kd),
+            hbm(2, 6, 2, hb, kd), hbm(tok, ff // 2),
         ]
         sem = pltpu.SemaphoreType.DMA
         scratch = [
@@ -905,9 +943,10 @@
             pltpu.VMEM((2, hb, kd), F32),
             pltpu.VMEM((2, hb, kd), BF16),
             pltpu.VMEM((8, hb, kd), BF16),
+            pltpu.VMEM((tok, ff // 2), BF16),
             sem((2,)), sem((2, 2, 7, SUB)), sem((2,)), sem((2, 8)), sem((2,)), sem((2, 11)), sem((blocks,)),
             sem((12,)), sem((2, 2, 4)), sem((4, 2, 2)), sem((2,)),
-            sem((2,)), sem((2,)), sem((2,)), sem((8,)), sem((2, 6, 2)), sem((2, 3)), sem((2, 2, 2)), sem((2,)), sem((4,)),
+            sem((2,)), sem((2,)), sem((2,)), sem((8,)), sem((2, 6, 2)), sem((2, 3)), sem((2, 2)), sem((2,)), sem((4,)), sem((8,)),
         ]
         res = pl.pallas_call(
             functools.partial(kernel, side),
@@ -920,7 +959,7 @@
             ),
             name="gated_mlp_backward",
         )(x, dy, gate, up, wg, wu, wd)
-        fins, rest, res = res[:2], res[2], res[3:6]
+        fins, rest, short, res = res[:2], res[2], res[3], res[4:7]
         moved = [lax.ppermute(v, ("dp", "tp"), way) for v, way in zip(fins, ways)]
         anywhere = [pl.BlockSpec(memory_space=pl.ANY)] * len(res)
         grads = pl.pallas_call(
@@ -934,7 +973,9 @@
             cost_estimate=pl.CostEstimate(flops=10**10, bytes_accessed=6 * d * ff * 2, transcendentals=0),
             name="copy_out",
         )(*res)
-        dx = (jnp.concatenate(moved).astype(F32) + rest).astype(BF16)
+        x, y = divmod(lax.axis_index("tp"), side)
+        swap = (lax.axis_index("dp") + (x + y) % side // 2) % 2
+        dx = (jnp.concatenate(moved).astype(F32) + jnp.where(swap == 1, short.astype(F32), rest)).astype(BF16)
         return dx, *grads
 
     rows, cols = P(("dp", "tp"), None), P("dp", "tp")

time: 469 us -> 466 us (level)
  no operation moved by 1% of the time
where the time goes in v4:
time: 466 us; the launch traced here: 465 us
  Pallas kernels  459 us (98%)
    pallas_call x1, Pallas kernels, local(): pl.pallas_call(functools.partial(kernel, side), out_shape=outs, in_specs=...  441 us
    pallas_call x1, Pallas kernels, local(): pl.pallas_call(copy_out, out_shape=[hbm(*v.shape) for v in res], in_specs...  17.8 us
  transfers between devices with their start and end apart: 2, of which 0 were waited for; matrix products, arithmetic and copies ran while one was open for 0% of the time, Pallas kernels for 4%

profile of v4, /device:TPU:97, one launch (start us, length us, event | category | flops | bytes accessed | tf_op | source)
XLA Modules:
  0.0 464.9 jit_solution(10972157133336152167)
XLA Ops:
  0.6 441.1 %gated_mlp_backward.1 = (bf16[128,4096]{1,0:T(8,128)(2,1)}, bf16[128,4096]{1,0:T(8,128)(2,1)}, f32[256,4096]{1,0:T(8,128)}, bf16[256,4096]{1,0:T(8,128)(2,1)}, b...) custom-call(bf16[256,4096]{1,0:T(8,128)(2,1)} %x_in.1, ...), custom_call_target="tpu_custom_call" | custom-call | tf_op jit(solution)/shard_map/gated_mlp_backward/pallas_call | solution.py:951
  441.7 2.1 collective-permute-start.1
  443.8 1.0 collective-permute-start
  444.8 0.0 copy-start
  444.8 0.0 copy-start.1
  444.8 17.8 %copy_out.1 = (bf16[4096,1024]{1,0:T(8,128)(2,1)}, bf16[4096,1024]{1,0:T(8,128)(2,1)}, bf16[1024,4096]{1,0:T(8,128)(2,1)}) custom-call(bf16[4096,1024]{1,0:T(8,128)(2,1)} %get-tuple-element.18.refs_0_, bf16[4096,1024]{1,0:T(8,128)(2,1)} %get-tuple-element.19.refs_1_, bf16[1024,4096]{1,0:T(8,128)(2,1)} %get-tuple-element.20.refs_2_), custom_call_target="tpu_custom_call" | custom-call | flops 10000000000 | bytes 50331648 | tf_op jit(solution)/shard_map/copy_out/pallas_call | solution.py:965
  462.6 0.0 collective-permute-done.1
  462.6 0.0 collective-permute-done
  462.6 0.0 copy-done
  462.6 0.0 copy-done.1
  462.6 2.2 add_convert_fusion
Async XLA Ops:
  441.7 20.9 %collective-permute-start.1 = (bf16[128,4096]{1,0:T(8,128)(2,1)}, bf16[128,4096]{1,0:T(8,128)(2,1)S(1)}, u32[]{:S(2)}, u32[]{:S(2)}) collective-permute-start(bf16[128,4096]{1,0:T(8,128)(2,1)} %get-tuple-element.15), channel_id=1, source_target_pairs={{0,4},{1,0},{2,17},{3,23},{4,7},{5,20},{6,26},{7,11},{8,27},{9,29}... | collective-permute-start | bytes 3145736 | tf_op jit(solution)/shard_map/ppermute | solution.py:963
  443.8 18.8 %collective-permute-start = (bf16[128,4096]{1,0:T(8,128)(2,1)}, bf16[128,4096]{1,0:T(8,128)(2,1)S(1)}, u32[]{:S(2)}, u32[]{:S(2)}) collective-permute-start(bf16[128,4096]{1,0:T(8,128)(2,1)} %get-tuple-element.14), channel_id=1, source_target_pairs={{0,1},{1,13},{2,30},{3,16},{4,0},{5,17},{6,23},{7,4},{8,20},{9,26}... | collective-permute-start | bytes 3145736 | tf_op jit(solution)/shard_map/ppermute | solution.py:963
  444.8 17.8 %copy-start = (f32[256,4096]{1,0:T(8,128)S(1)}, f32[256,4096]{1,0:T(8,128)}, u32[]{:S(2)}) copy-start(f32[256,4096]{1,0:T(8,128)} %get-tuple-element.17) | copy-start | bytes 12582916
  444.8 17.8 %copy-start.1 = (bf16[256,4096]{1,0:T(8,128)(2,1)S(1)}, bf16[256,4096]{1,0:T(8,128)(2,1)}, u32[]{:S(2)}) copy-start(bf16[256,4096]{1,0:T(8,128)(2,1)} %get-tuple-element.16) | copy-start | bytes 6291460

commit v5 on v4

--- a/solution.py
+++ b/solution.py
@@ -25,7 +25,7 @@
 DY_AT = ((2, 4, 6, 8, 10), (2, 6, 8, 10, NEVER))
 X_START = (10, 10)
 X_AT = (
-    (12, 12, 16, 18, 23, 27, 32, 36, 41, 45, 50, 55),
+    (12, 12, 16, 17, 21, 25, 30, 34, 39, 43, 48, 53),
     (13, 15, 18, 21, 25, 30, 34, 38, 43, 48, 52, 55),
 )
 SUMS_AT = (55, 49)
@@ -719,39 +719,6 @@
 
     rs_start(1)
     rs_short(1)
-    pl.when(swap == 1)(lambda: dy_wait(2))
-    for half_of in BOTH:
-        q = 2 + half_of
-        if half_of:
-
-            @on_stay
-            def _():
-                for dn in BOTH:
-                    rest_put(dn, 0)
-
-            pl.when(swap == 1)(lambda: dy_wait(q))
-
-        @pl.loop(0, 2)
-        def _(i):
-            tt = 2 * half_of + i
-            rs_take(tt, 0)
-
-            @on_stay
-            def _():
-                down_out(2, tt, od).wait()
-                down_put(3, tt, tt)
-                down_out(3, tt, od).start()
-
-            @on_swap
-            def _():
-                down_put(q, 2 * i, 2 * i + half_of)
-                down_remote(q, i).start()
-
-            rs_give(tt, 0)
-
-    for i in range(8):
-        d2d_wait(1, i)
-
     def x_cols(i, th):
         slot = lax.rem(i, 4)
         return pltpu.make_async_copy(
@@ -764,6 +731,40 @@
         for th in BOTH:
             x_cols(i, th).start()
 
+    pl.when(swap == 1)(lambda: dy_wait(2))
+    for half_of in BOTH:
+        q = 2 + half_of
+        if half_of:
+
+            @on_stay
+            def _():
+                for dn in BOTH:
+                    rest_put(dn, 0)
+
+            pl.when(swap == 1)(lambda: dy_wait(q))
+            for i in range(8):
+                d2d_wait(1, i)
+            for i in range(3):
+                x_start(i)
+
+        @pl.loop(0, 2)
+        def _(i):
+            tt = 2 * half_of + i
+            rs_take(tt, 0)
+
+            @on_stay
+            def _():
+                down_out(2, tt, od).wait()
+                down_put(3, tt, tt)
+                down_out(3, tt, od).start()
+
+            @on_swap
+            def _():
+                down_put(q, 2 * i, 2 * i + half_of)
+                down_remote(q, i).start()
+
+            rs_give(tt, 0)
+
     def dw_local(i, a):
         o = lax.rem(i, 4)
         return pltpu.make_async_copy(out.at[o, a], (og, ou)[a].at[pl.ds(al(i * rb, rb), rb), :], osem.at[o, a, 0])
@@ -794,9 +795,6 @@
         def _():
             for l in BOTH:
                 dw_remote(i, a, l).wait_send()
-
-    for i in range(3):
-        x_start(i)
 
     @on_stay
     def _():

time: 466 us -> 466 us (level)
  no operation moved by 1% of the time
where the time goes in v5:
time: 466 us; the launch traced here: 465 us
  Pallas kernels  459 us (98%)
    pallas_call x1, Pallas kernels, local(): pl.pallas_call(functools.partial(kernel, side), out_shape=outs, in_specs=...  441 us
    pallas_call x1, Pallas kernels, local(): pl.pallas_call(copy_out, out_shape=[hbm(*v.shape) for v in res], in_specs...  17.8 us
  transfers between devices with their start and end apart: 2, of which 0 were waited for; matrix products, arithmetic and copies ran while one was open for 0% of the time, Pallas kernels for 4%

profile of v5, /device:TPU:97, one launch (start us, length us, event | category | flops | bytes accessed | tf_op | source)
XLA Modules:
  0.0 464.8 jit_solution(7094253172327816851)
XLA Ops:
  0.6 441.1 %gated_mlp_backward.1 = (bf16[128,4096]{1,0:T(8,128)(2,1)}, bf16[128,4096]{1,0:T(8,128)(2,1)}, f32[256,4096]{1,0:T(8,128)}, bf16[256,4096]{1,0:T(8,128)(2,1)}, b...) custom-call(bf16[256,4096]{1,0:T(8,128)(2,1)} %x_in.1, ...), custom_call_target="tpu_custom_call" | custom-call | tf_op jit(solution)/shard_map/gated_mlp_backward/pallas_call | solution.py:949
  441.7 2.1 collective-permute-start.1
  443.8 0.9 collective-permute-start
  444.8 0.0 copy-start
  444.8 0.0 copy-start.1
  444.8 17.8 %copy_out.1 = (bf16[4096,1024]{1,0:T(8,128)(2,1)}, bf16[4096,1024]{1,0:T(8,128)(2,1)}, bf16[1024,4096]{1,0:T(8,128)(2,1)}) custom-call(bf16[4096,1024]{1,0:T(8,128)(2,1)} %get-tuple-element.18.refs_0_, bf16[4096,1024]{1,0:T(8,128)(2,1)} %get-tuple-element.19.refs_1_, bf16[1024,4096]{1,0:T(8,128)(2,1)} %get-tuple-element.20.refs_2_), custom_call_target="tpu_custom_call" | custom-call | flops 10000000000 | bytes 50331648 | tf_op jit(solution)/shard_map/copy_out/pallas_call | solution.py:963
  462.6 0.0 collective-permute-done.1
  462.6 0.0 collective-permute-done
  462.6 0.0 copy-done
  462.6 0.0 copy-done.1
  462.6 2.2 add_convert_fusion
Async XLA Ops:
  441.7 20.9 %collective-permute-start.1 = (bf16[128,4096]{1,0:T(8,128)(2,1)}, bf16[128,4096]{1,0:T(8,128)(2,1)S(1)}, u32[]{:S(2)}, u32[]{:S(2)}) collective-permute-start(bf16[128,4096]{1,0:T(8,128)(2,1)} %get-tuple-element.15), channel_id=1, source_target_pairs={{0,4},{1,0},{2,17},{3,23},{4,7},{5,20},{6,26},{7,11},{8,27},{9,29}... | collective-permute-start | bytes 3145736 | tf_op jit(solution)/shard_map/ppermute | solution.py:961
  443.8 18.8 %collective-permute-start = (bf16[128,4096]{1,0:T(8,128)(2,1)}, bf16[128,4096]{1,0:T(8,128)(2,1)S(1)}, u32[]{:S(2)}, u32[]{:S(2)}) collective-permute-start(bf16[128,4096]{1,0:T(8,128)(2,1)} %get-tuple-element.14), channel_id=1, source_target_pairs={{0,1},{1,13},{2,30},{3,16},{4,0},{5,17},{6,23},{7,4},{8,20},{9,26}... | collective-permute-start | bytes 3145736 | tf_op jit(solution)/shard_map/ppermute | solution.py:961
  444.8 17.8 %copy-start = (f32[256,4096]{1,0:T(8,128)S(1)}, f32[256,4096]{1,0:T(8,128)}, u32[]{:S(2)}) copy-start(f32[256,4096]{1,0:T(8,128)} %get-tuple-element.17) | copy-start | bytes 12582916
  444.8 17.8 %copy-start.1 = (bf16[256,4096]{1,0:T(8,128)(2,1)S(1)}, bf16[256,4096]{1,0:T(8,128)(2,1)}, u32[]{:S(2)}) copy-start(bf16[256,4096]{1,0:T(8,128)(2,1)} %get-tuple-element.16) | copy-start | bytes 6291460
